TPU v7x, 32 devices: a whole 2x2x4 slice. The times are simulated.
32 devices in a mesh: dp: 2 (over x), tp: 4 (over z), sp: 4 (over y, core).
Axes of the slice: x: 2, y: 2, z: 4, core: 2. Of those that a mesh axis runs over, the one named last changes fastest.
Arguments:
- x_seq: bfloat16 [16384, 2304], P(('dp', 'sp', 'tp')), parts along dimension 0
- w_query: bfloat16 [2304, 8, 256], P(None, 'tp')
- w_key: bfloat16 [2304, 4, 256], P(None, 'tp')
- w_value: bfloat16 [2304, 4, 256], P(None, 'tp')
- w_out: bfloat16 [8, 256, 2304], P('tp')
Outputs:
- output: bfloat16 [16384, 2304], P(('dp', 'sp', 'tp')), parts along dimension 0
There are 2 independent parts. A program takes and returns all parts, laid end to end along the dimension named above; an argument that names none is the same for every part.
All inputs are finite; a program needn't handle non-finite values.
Results may differ from a plain program's by a relative error of at most 0.00549951.
Values are sent between devices in bfloat16 or wider.
A program may use at most 1 GiB of HBM per device.

v0:
```python
import jax
import jax.numpy as jnp
from jax import lax
from jax.sharding import PartitionSpec as P

WINDOW = 4096
NEG_BIG = -1e30


def block_update(soft_state, q_blk, k_blk, v_blk, chunk_gap, score_scale):
    row_max, row_sum, acc_sum = soft_state
    chunk_len = q_blk.shape[0]
    scores = jnp.einsum("qhgd,khd->hgqk", q_blk, k_blk, preferred_element_type=jnp.float32) * score_scale
    offset = chunk_gap * chunk_len + lax.broadcasted_iota(jnp.int32, (chunk_len, chunk_len), 0) - lax.broadcasted_iota(jnp.int32, (chunk_len, chunk_len), 1)
    visible = (offset >= 0) & (offset < WINDOW)
    scores = jnp.where(visible, scores, NEG_BIG)
    new_max = jnp.maximum(row_max, jnp.max(scores, axis=-1))
    prob_blk = jnp.where(visible, jnp.exp(scores - new_max[..., None]), 0.0)
    rescale = jnp.exp(row_max - new_max)
    new_sum = row_sum * rescale + jnp.sum(prob_blk, axis=-1)
    new_acc = acc_sum * rescale[..., None] + jnp.einsum("hgqk,khd->hgqd", prob_blk.astype(jnp.bfloat16), v_blk, preferred_element_type=jnp.float32)
    return new_max, new_sum, new_acc


def pair_update(soft_state, q_blk, k_blk, v_blk, q_id, k_id, score_scale):
    chunk_len = q_blk.shape[0]
    chunk_gap = q_id - k_id
    needed = (chunk_gap >= 0) & (chunk_gap * chunk_len - chunk_len + 1 < WINDOW)
    return lax.cond(needed, lambda cur_state: block_update(cur_state, q_blk, k_blk, v_blk, chunk_gap, score_scale), lambda cur_state: cur_state, soft_state)


def solution(mesh):
    sp_size = mesh.shape["sp"]
    next_pairs = [(src_idx, (src_idx + 1) % sp_size) for src_idx in range(sp_size)]

    def local_attn(x_part, w_query, w_key, w_value, w_out):
        x_block = lax.all_gather(x_part, "tp", axis=0, tiled=True)
        block_rows, d_model = x_block.shape
        chunk_len = block_rows // 2
        heads_loc, head_dim = w_query.shape[1], w_query.shape[2]
        kv_loc = w_key.shape[1]
        group_size = heads_loc // kv_loc
        score_scale = head_dim ** -0.5
        q_loc = jnp.dot(x_block, w_query.reshape(d_model, heads_loc * head_dim), preferred_element_type=jnp.float32).astype(jnp.bfloat16).reshape(2, chunk_len, kv_loc, group_size, head_dim)
        k_loc = jnp.dot(x_block, w_key.reshape(d_model, kv_loc * head_dim), preferred_element_type=jnp.float32).astype(jnp.bfloat16).reshape(2, chunk_len, kv_loc, head_dim)
        v_loc = jnp.dot(x_block, w_value.reshape(d_model, kv_loc * head_dim), preferred_element_type=jnp.float32).astype(jnp.bfloat16).reshape(2, chunk_len, kv_loc, head_dim)
        sp_rank = lax.axis_index("sp")
        own_ids = (sp_rank, 2 * sp_size - 1 - sp_rank)

        def fresh_state():
            return (jnp.full((kv_loc, group_size, chunk_len), NEG_BIG, jnp.float32), jnp.zeros((kv_loc, group_size, chunk_len), jnp.float32), jnp.zeros((kv_loc, group_size, chunk_len, head_dim), jnp.float32))

        def absorb(states, k_blocks, v_blocks, src_rank):
            key_ids = (src_rank, 2 * sp_size - 1 - src_rank)
            updated = []
            for q_half in range(2):
                cur_state = states[q_half]
                for k_half in range(2):
                    cur_state = pair_update(cur_state, q_loc[q_half], k_blocks[k_half], v_blocks[k_half], own_ids[q_half], key_ids[k_half], score_scale)
                updated.append(cur_state)
            return tuple(updated)

        states = absorb((fresh_state(), fresh_state()), k_loc, v_loc, sp_rank)

        def ring_free_step(step_idx, carry):
            k_blocks, v_blocks, cur_states = carry
            k_blocks, v_blocks = lax.ppermute((k_blocks, v_blocks), "sp", next_pairs)
            src_rank = (sp_rank - step_idx) % sp_size
            return k_blocks, v_blocks, absorb(cur_states, k_blocks, v_blocks, src_rank)

        carry_out = lax.fori_loop(1, sp_size, ring_free_step, (k_loc, v_loc, states))
        states = carry_out[2]
        outs_norm = jnp.stack([(soft_state[2] / soft_state[1][..., None]).astype(jnp.bfloat16) for soft_state in states])
        part_sum = jnp.einsum("ahgqd,hgde->aqe", outs_norm, w_out.reshape(kv_loc, group_size, head_dim, d_model), preferred_element_type=jnp.float32).reshape(block_rows, d_model)
        y_rows = lax.psum_scatter(part_sum, "tp", scatter_dimension=0, tiled=True)
        return y_rows.astype(jnp.bfloat16)

    return jax.shard_map(local_attn, mesh=mesh, in_specs=(P(("dp", "sp", "tp"), None), P(None, "tp", None), P(None, "tp", None), P(None, "tp", None), P("tp", None, None)), out_specs=P(("dp", "sp", "tp"), None), check_vma=False)
```

profile of v0, /device:TPU:26, one launch (start us, length us, event | category | flops | bytes accessed | tf_op | source)
XLA Modules:
  0.0 763.7 jit_solution(7325641846916408201)
XLA Ops:
  7.3 3.5 copy.38
  11.1 163.0 %all-gather.2.cloned.1.call-done = bf16[2048,2304]{1,0:T(8,128)(2,1)} async-done(((bf16[512,2304]{1,0:T(8,128)(2,1)}), bf16[2048,2304]{1,0:T(8,128)(2,1)}) %all-gather.2.cloned.1.call-update) | async-done | bytes 9437200 | tf_op jit(solution)/shard_map/all_gather | solution.py:37
  174.1 8.4 %convolution_convert_fusion = bf16[2048,512]{0,1:T(8,128)(2,1)S(1)} fusion(bf16[2048,2304]{1,0:T(8,128)(2,1)} %all-gather.2.cloned.1.call-done, bf16[2304,512]{1,0:T(8,128)(2,1)} %bitcast.414), kind=kOutput, calls=%fused_computation.175 | convolution fusion | flops 4832886784 | bytes 13893632 | tf_op jit(solution)/shard_map/dot_general | solution.py:44
  182.6 1.3 copy-done.7
  183.9 1.6 fusion.162
  185.4 4.5 reshape.333
  189.9 6.7 convolution_convert_fusion.1
  196.6 6.7 convolution_convert_fusion.2
  203.4 1.4 fusion.163
  204.8 1.3 fusion.147
  206.1 7.1 fusion.119
  213.2 1.7 conditional.7
  213.2 1.5 broadcast.235
  214.9 8.1 %fusion.123 = (f32[2,1024]{1,0:T(2,128)S(1)}, f32[2,1024]{1,0:T(2,128)S(1)}) fusion(f32[1024,1024,2]{1,0,2:T(8,128)} %get-tuple-element.771, f32[2,1024]{1,0:T(2,128)S(1)} %bitcast.401, pred[1024,1024]{0,1:T(8,128)(4,1)S(1)} %fusion.132, f32[2,1024]{1,0:T(2,128)S(1)} %get-tuple-element.770, f32[1024,1024,2]{1,0,2:T(8,128)} %copy-done.1), kind=kLoop, calls=%fused_computation.164 | loop fusion | flops 20967424 | bytes 17858560 | tf_op jit(solution)/shard_map/cond/branch_1_fun/reduce_sum | solution.py:20
  223.4 4.0 add_bitcast_fusion.1
  227.4 6.1 copy.22
  233.5 8.3 %bitcast_add_fusion.11 = f32[1,2,1024,256]{3,2,1,0:T(8,128)} fusion(f32[1,2,1024,256]{3,2,1,0:T(8,128)} %get-tuple-element.672, f32[1024,1024,2]{1,0,2:T(8,128)} %get-tuple-element.771, f32[2,1024]{1,0:T(2,128)S(1)} %bitcast.402, pred[1024,1024]{0,1:T(8,128)(4,1)S(1)} %fusion.132, f32[2,1024]{1,0:T(2,128)S(1)} %get-tuple-element.740, ...), kind=kOutput, calls=%fused_computation.179 | convolution fusion | flops 1085276160 | bytes 14172160 | tf_op jit(solution)/shard_map/cond/branch_1_fun/hgqk,khd->hgqd/dot_general | solution.py:21
  241.8 171.0 %while.32 = (s32[]{:T(128)}, bf16[2,1024,1,256]{3,1,2,0:T(8,128)(2,1)}, bf16[2,1024,1,256]{3,1,2,0:T(8,128)(2,1)}, f32[1,2,1024]{2,1,0:T(2,128)S(1)}, f32[1,2,10...) while((s32[]{:T(128)}, ...), condition=%wide.region_29.30_spmd, body=%wide.region_12.29_spmd.sunk | while | flops 8719986688 | bytes 239633840 | solution.py:71
  256.3 10.8 %collective-permute-start.1 = (bf16[2,1024,1,256]{3,1,2,0:T(8,128)(2,1)}, bf16[2,1024,1,256]{3,1,2,0:T(8,128)(2,1)}, u32[]{:S(2)}, u32[]{:S(2)}) collective-permute-start(bf16[2,1024,1,256]{3,1,2,0:T(8,128)(2,1)} %get-tuple-element.941), channel_id=1, source_target_pairs={{0,1},{1,2},{2,3},{3,0},{4,5},{5,6},{6,7},{7,4},{8,9},{9,10},{10,1... | collective-permute-start | bytes 3145736 | tf_op jit(solution)/shard_map/while/body/eval_jaxpr/ppermute | solution.py:67
  267.2 3.0 slice_bitcast_fusion.10
  270.2 8.8 %collective-permute-done = bf16[2,1024,1,256]{3,1,2,0:T(8,128)(2,1)S(1)} collective-permute-done((bf16[2,1024,1,256]{3,1,2,0:T(8,128)(2,1)}, bf16[2,1024,1,256]{3,1,2,0:T(8,128)(2,1)S(1)}, u32[]{:S(2)}, u32[]{:S(2)}) %collective-permute-start) | collective-permute-done | bytes 1048608 | tf_op jit(solution)/shard_map/while/body/eval_jaxpr/ppermute | solution.py:67
  280.1 10.2 %collective-permute-done.1 = bf16[2,1024,1,256]{3,1,2,0:T(8,128)(2,1)} collective-permute-done((bf16[2,1024,1,256]{3,1,2,0:T(8,128)(2,1)}, bf16[2,1024,1,256]{3,1,2,0:T(8,128)(2,1)}, u32[]{:S(2)}, u32[]{:S(2)}) %collective-permute-start.1) | collective-permute-done | bytes 1048608 | tf_op jit(solution)/shard_map/while/body/eval_jaxpr/ppermute | solution.py:67
  290.3 2.2 slice_bitcast_fusion.11
  292.5 11.5 %conditional.14 = ((f32[1,2,1024]{2,1,0:T(2,128)S(1)}, f32[1,2,1024]{2,1,0:T(2,128)S(1)}, f32[1,2,1024,256]{3,2,1,0:T(8,128)})) conditional(s32[]{:T(128)} %convert_element_type.180, (f32[1,2,1024]{2,1,0:T(2,128)S(1)}, f32[1,2,1024]{2,1,0:T(2,128)S(1)}, f32[1,2,1024,256]{3,2,1,0:T(8,128)}) %tuple.140, (s32[]{:T(128)}, ...), branch_computations={%region_21.21_spmd, %region_22.0_spmd} | conditional | flops 2179996672 | bytes 54665348 | solution.py:29
  292.5 1.1 fusion.86
  293.7 3.2 fusion.78
  296.9 2.3 fusion.80
  299.2 3.4 bitcast_add_fusion.7
  302.7 1.3 copy-done.11
  304.0 11.5 %conditional.15 = ((f32[1,2,1024]{2,1,0:T(2,128)S(1)}, f32[1,2,1024]{2,1,0:T(2,128)S(1)}, f32[1,2,1024,256]{3,2,1,0:T(8,128)})) conditional(s32[]{:T(128)} %convert_element_type.179, (f32[1,2,1024]{2,1,0:T(2,128)S(1)}, f32[1,2,1024]{2,1,0:T(2,128)S(1)}, f32[1,2,1024,256]{3,2,1,0:T(8,128)}) %get-tuple-element.982, (s32[]{:T(128)}, ...), branch_computations={%region_25.25_spmd, %region_26.0_spmd} | conditional | flops 2179996672 | bytes 54665348 | solution.py:29
  305.1 3.2 fusion.98
  308.4 2.3 fusion.100
  310.7 3.4 bitcast_add_fusion.9
  314.2 1.3 copy-done.13
  316.5 2.3 copy.95
  318.7 2.4 collective-permute-start.1
  321.1 3.0 slice_bitcast_fusion.10
  324.2 8.8 %collective-permute-done = bf16[2,1024,1,256]{3,1,2,0:T(8,128)(2,1)S(1)} collective-permute-done((bf16[2,1024,1,256]{3,1,2,0:T(8,128)(2,1)}, bf16[2,1024,1,256]{3,1,2,0:T(8,128)(2,1)S(1)}, u32[]{:S(2)}, u32[]{:S(2)}) %collective-permute-start) | collective-permute-done | bytes 1048608 | tf_op jit(solution)/shard_map/while/body/eval_jaxpr/ppermute | solution.py:67
  334.0 10.2 %collective-permute-done.1 = bf16[2,1024,1,256]{3,1,2,0:T(8,128)(2,1)} collective-permute-done((bf16[2,1024,1,256]{3,1,2,0:T(8,128)(2,1)}, bf16[2,1024,1,256]{3,1,2,0:T(8,128)(2,1)}, u32[]{:S(2)}, u32[]{:S(2)}) %collective-permute-start.1) | collective-permute-done | bytes 1048608 | tf_op jit(solution)/shard_map/while/body/eval_jaxpr/ppermute | solution.py:67
  344.2 2.2 slice_bitcast_fusion.11
  346.4 11.5 %conditional.15 = ((f32[1,2,1024]{2,1,0:T(2,128)S(1)}, f32[1,2,1024]{2,1,0:T(2,128)S(1)}, f32[1,2,1024,256]{3,2,1,0:T(8,128)})) conditional(s32[]{:T(128)} %convert_element_type.179, (f32[1,2,1024]{2,1,0:T(2,128)S(1)}, f32[1,2,1024]{2,1,0:T(2,128)S(1)}, f32[1,2,1024,256]{3,2,1,0:T(8,128)}) %get-tuple-element.982, (s32[]{:T(128)}, ...), branch_computations={%region_25.25_spmd, %region_26.0_spmd} | conditional | flops 2179996672 | bytes 54665348 | solution.py:29
  346.5 1.1 fusion.106
  347.6 3.2 fusion.98
  350.9 2.3 fusion.100
  353.2 3.4 bitcast_add_fusion.9
  356.6 1.3 copy-done.13
  358.9 2.3 copy.95
  361.2 11.4 %collective-permute-start = (bf16[2,1024,1,256]{3,1,2,0:T(8,128)(2,1)}, bf16[2,1024,1,256]{3,1,2,0:T(8,128)(2,1)S(1)}, u32[]{:S(2)}, u32[]{:S(2)}) collective-permute-start(bf16[2,1024,1,256]{3,1,2,0:T(8,128)(2,1)} %get-tuple-element.940), channel_id=1, source_target_pairs={{0,1},{1,2},{2,3},{3,0},{4,5},{5,6},{6,7},{7,4},{8,9},{9,10},{10,1... | collective-permute-start | bytes 3145736 | tf_op jit(solution)/shard_map/while/body/eval_jaxpr/ppermute | solution.py:67
  372.6 3.0 slice_bitcast_fusion.10
  375.6 8.8 %collective-permute-done = bf16[2,1024,1,256]{3,1,2,0:T(8,128)(2,1)S(1)} collective-permute-done((bf16[2,1024,1,256]{3,1,2,0:T(8,128)(2,1)}, bf16[2,1024,1,256]{3,1,2,0:T(8,128)(2,1)S(1)}, u32[]{:S(2)}, u32[]{:S(2)}) %collective-permute-start) | collective-permute-done | bytes 1048608 | tf_op jit(solution)/shard_map/while/body/eval_jaxpr/ppermute | solution.py:67
  385.5 10.2 %collective-permute-done.1 = bf16[2,1024,1,256]{3,1,2,0:T(8,128)(2,1)} collective-permute-done((bf16[2,1024,1,256]{3,1,2,0:T(8,128)(2,1)}, bf16[2,1024,1,256]{3,1,2,0:T(8,128)(2,1)}, u32[]{:S(2)}, u32[]{:S(2)}) %collective-permute-start.1) | collective-permute-done | bytes 1048608 | tf_op jit(solution)/shard_map/while/body/eval_jaxpr/ppermute | solution.py:67
  395.7 2.2 slice_bitcast_fusion.11
  397.9 11.5 %conditional.15 = ((f32[1,2,1024]{2,1,0:T(2,128)S(1)}, f32[1,2,1024]{2,1,0:T(2,128)S(1)}, f32[1,2,1024,256]{3,2,1,0:T(8,128)})) conditional(s32[]{:T(128)} %convert_element_type.179, (f32[1,2,1024]{2,1,0:T(2,128)S(1)}, f32[1,2,1024]{2,1,0:T(2,128)S(1)}, f32[1,2,1024,256]{3,2,1,0:T(8,128)}) %get-tuple-element.982, (s32[]{:T(128)}, ...), branch_computations={%region_25.25_spmd, %region_26.0_spmd} | conditional | flops 2179996672 | bytes 54665348 | solution.py:29
  397.9 1.1 fusion.106
  399.1 3.2 fusion.98
  402.3 2.3 fusion.100
  404.6 3.4 bitcast_add_fusion.9
  408.1 1.3 copy-done.13
  410.4 2.3 copy.95
  412.9 1.9 fusion.141
  414.8 1.9 fusion.142
  417.1 9.5 %convolution_bitcast_fusion = f32[2048,2304]{1,0:T(8,128)} fusion(bf16[2048,256,2]{1,0,2:T(8,128)(2,1)S(1)} %bitcast.416, bf16[2,256,2304]{2,1,0:T(8,128)(2,1)S(1)} %copy-done), kind=kOutput, calls=%fused_computation.154 | convolution fusion | flops 4831838208 | bytes 23330816 | tf_op jit(solution)/shard_map/ahgqd,hgde->aqe/dot_general | solution.py:74
  426.6 325.8 %reduce-scatter.2.cloned.1.call-done = f32[512,2304]{1,0:T(8,128)} async-done(((f32[2048,2304]{1,0:T(8,128)}), f32[512,2304]{1,0:T(8,128)}) %reduce-scatter.2.cloned.1.call-update) | async-done | bytes 4718608 | tf_op jit(solution)/shard_map/reduce_scatter | solution.py:75
  752.5 4.0 convert_element_type.115
  (85 shorter events, 9.5 us)
Async XLA Ops:
  6.5 410.6 %copy-start = (bf16[2,256,2304]{2,1,0:T(8,128)(2,1)S(1)}, bf16[2,256,2304]{2,1,0:T(8,128)(2,1)}, u32[]{:S(2)}) copy-start(bf16[2,256,2304]{2,1,0:T(8,128)(2,1)} %param.23) | copy-start | bytes 7077892
  6.5 167.6 %all-gather.2.cloned.1.call-start = ((), (), s32[]{:S(2)}) async-start(), calls=%async_computation.1 | async-start | bytes 11796480 | tf_op jit(solution)/shard_map/all_gather | solution.py:37
  7.3 745.2 %reduce-scatter.2.cloned.1.call-start = ((), (), s32[]{:S(2)}) async-start(), calls=%async_computation.2 | async-start | bytes 23592960 | tf_op jit(solution)/shard_map/reduce_scatter | solution.py:75
  182.6 1.3 copy-start.7
  189.9 6.7 copy-start.24
  196.6 6.7 copy-start.20
  196.6 8.2 %copy-start.8 = (bf16[1024,512]{0,1:T(8,128)(2,1)S(1)}, bf16[1024,512]{0,1:T(8,128)(2,1)}, u32[]{:S(2)}) copy-start(bf16[1024,512]{0,1:T(8,128)(2,1)} %get-tuple-element.762) | copy-start | bytes 3145732
  203.3 9.8 %copy-start.9 = (bf16[2048,256]{1,0:T(8,128)(2,1)}, bf16[2048,256]{1,0:T(8,128)(2,1)S(1)}, u32[]{:S(2)}) copy-start(bf16[2048,256]{1,0:T(8,128)(2,1)S(1)} %convolution_convert_fusion.2) | copy-start | bytes 3145732
  206.1 7.1 copy-start.1
  214.9 8.2 %copy-start.2 = (f32[1024,1024,2]{1,0,2:T(8,128)S(1)}, f32[1024,1024,2]{1,0,2:T(8,128)}, u32[]{:S(2)}) copy-start(f32[1024,1024,2]{1,0,2:T(8,128)} %copy-done.1) | copy-start | bytes 25165828
  214.9 8.4 %copy-start.21 = (bf16[2048,256]{1,0:T(8,128)(2,1)S(1)}, bf16[2048,256]{1,0:T(8,128)(2,1)}, u32[]{:S(2)}) copy-start(bf16[2048,256]{1,0:T(8,128)(2,1)} %copy-done.20) | copy-start | bytes 3145732
  256.3 22.8 %collective-permute-start = (bf16[2,1024,1,256]{3,1,2,0:T(8,128)(2,1)}, bf16[2,1024,1,256]{3,1,2,0:T(8,128)(2,1)S(1)}, u32[]{:S(2)}, u32[]{:S(2)}) collective-permute-start(bf16[2,1024,1,256]{3,1,2,0:T(8,128)(2,1)} %get-tuple-element.940), channel_id=1, source_target_pairs={{0,1},{1,2},{2,3},{3,0},{4,5},{5,6},{6,7},{7,4},{8,9},{9,10},{10,1... | collective-permute-start | bytes 3145736 | tf_op jit(solution)/shard_map/while/body/eval_jaxpr/ppermute | solution.py:67
  256.3 33.9 %collective-permute-start.1 = (bf16[2,1024,1,256]{3,1,2,0:T(8,128)(2,1)}, bf16[2,1024,1,256]{3,1,2,0:T(8,128)(2,1)}, u32[]{:S(2)}, u32[]{:S(2)}) collective-permute-start(bf16[2,1024,1,256]{3,1,2,0:T(8,128)(2,1)} %get-tuple-element.941), channel_id=1, source_target_pairs={{0,1},{1,2},{2,3},{3,0},{4,5},{5,6},{6,7},{7,4},{8,9},{9,10},{10,1... | collective-permute-start | bytes 3145736 | tf_op jit(solution)/shard_map/while/body/eval_jaxpr/ppermute | solution.py:67
  296.9 2.3 copy-start.5
  296.9 2.3 copy-start.10
  302.7 1.3 copy-start.11
  308.4 2.3 copy-start.3
  308.4 2.3 copy-start.12
  314.1 1.3 copy-start.13
  318.7 14.2 %collective-permute-start = (bf16[2,1024,1,256]{3,1,2,0:T(8,128)(2,1)}, bf16[2,1024,1,256]{3,1,2,0:T(8,128)(2,1)S(1)}, u32[]{:S(2)}, u32[]{:S(2)}) collective-permute-start(bf16[2,1024,1,256]{3,1,2,0:T(8,128)(2,1)} %get-tuple-element.940), channel_id=1, source_target_pairs={{0,1},{1,2},{2,3},{3,0},{4,5},{5,6},{6,7},{7,4},{8,9},{9,10},{10,1... | collective-permute-start | bytes 3145736 | tf_op jit(solution)/shard_map/while/body/eval_jaxpr/ppermute | solution.py:67
  318.7 25.5 %collective-permute-start.1 = (bf16[2,1024,1,256]{3,1,2,0:T(8,128)(2,1)}, bf16[2,1024,1,256]{3,1,2,0:T(8,128)(2,1)}, u32[]{:S(2)}, u32[]{:S(2)}) collective-permute-start(bf16[2,1024,1,256]{3,1,2,0:T(8,128)(2,1)} %get-tuple-element.941), channel_id=1, source_target_pairs={{0,1},{1,2},{2,3},{3,0},{4,5},{5,6},{6,7},{7,4},{8,9},{9,10},{10,1... | collective-permute-start | bytes 3145736 | tf_op jit(solution)/shard_map/while/body/eval_jaxpr/ppermute | solution.py:67
  350.8 2.3 copy-start.3
  350.8 2.3 copy-start.12
  356.6 1.3 copy-start.13
  361.2 23.2 %collective-permute-start = (bf16[2,1024,1,256]{3,1,2,0:T(8,128)(2,1)}, bf16[2,1024,1,256]{3,1,2,0:T(8,128)(2,1)S(1)}, u32[]{:S(2)}, u32[]{:S(2)}) collective-permute-start(bf16[2,1024,1,256]{3,1,2,0:T(8,128)(2,1)} %get-tuple-element.940), channel_id=1, source_target_pairs={{0,1},{1,2},{2,3},{3,0},{4,5},{5,6},{6,7},{7,4},{8,9},{9,10},{10,1... | collective-permute-start | bytes 3145736 | tf_op jit(solution)/shard_map/while/body/eval_jaxpr/ppermute | solution.py:67
  372.6 23.1 %collective-permute-start.1 = (bf16[2,1024,1,256]{3,1,2,0:T(8,128)(2,1)}, bf16[2,1024,1,256]{3,1,2,0:T(8,128)(2,1)}, u32[]{:S(2)}, u32[]{:S(2)}) collective-permute-start(bf16[2,1024,1,256]{3,1,2,0:T(8,128)(2,1)} %get-tuple-element.941), channel_id=1, source_target_pairs={{0,1},{1,2},{2,3},{3,0},{4,5},{5,6},{6,7},{7,4},{8,9},{9,10},{10,1... | collective-permute-start | bytes 3145736 | tf_op jit(solution)/shard_map/while/body/eval_jaxpr/ppermute | solution.py:67
  402.3 2.3 copy-start.3
  402.3 2.3 copy-start.12
  408.1 1.3 copy-start.13
Sparse Core Ops, SparseCore 0:
  8.9 165.1 all-gather.1
  426.8 325.6 reduce-scatter.1
where the time goes:
time: 775 us; the launch traced here: 764 us
  waiting for transfers between devices  546 us (70%)
  matrix products  78.5 us (10%)
  local copies, waits for them, and re-layouts  54.5 us (7%)
  other arithmetic  30.3 us (4%)
  starting transfers between devices  24.7 us (3%)
  loops' own time  15.3 us (2%)
  between operations  14 us (2%)
    reduce_scatter x1, waiting for transfers between devices, local_attn(): y_rows = lax.psum_scatter(part_sum, 'tp', scatter_dimension=0, tiled=True)  326 us
    all_gather x1, waiting for transfers between devices, local_attn(): x_block = lax.all_gather(x_part, 'tp', axis=0, tiled=True)  163 us
    ppermute x6, waiting for transfers between devices, ring_free_step(): k_blocks, v_blocks = lax.ppermute((k_blocks, v_blocks), 'sp', next_pairs)  56.9 us
    dot_general x6, matrix products, block_update(): jnp.einsum('hgqk,khd->hgqd', prob_blk.astype(jnp.bfloat16), v_blk, prefer...  26 us
    ppermute x6, starting transfers between devices, ring_free_step(): k_blocks, v_blocks = lax.ppermute((k_blocks, v_blocks), 'sp', next_pairs)  24.7 us
    dot_general x6, matrix products, block_update(): jnp.einsum('qhgd,khd->hgqk', q_blk, k_blk, preferred_element_type=jnp.flo...  21.2 us
    reduce_sum x5, other arithmetic, block_update(): new_sum = row_sum * rescale + jnp.sum(prob_blk, axis=-1)  17.1 us
  transfers between devices with their start and end apart: 8, of which 8 were waited for; matrix products, arithmetic and copies ran while one was open for 2% of the time, Pallas kernels for 0%

commit v1 on v0

v1 whole, which is shorter than its diff:
```python
import jax
import jax.numpy as jnp
from jax import lax
from jax.experimental import pallas as pl
from jax.experimental.pallas import tpu as pltpu
from jax.sharding import PartitionSpec as P


LOG2E = 1.4426950408889634


HB = 512
HD = 256
NSUB = 4


def attn_kernel(info_ref, *refs):
    q_in, q_shipped, kv_in = refs[:4], refs[4:7], refs[7:23]
    o_ref = refs[23]
    q_all, kv_all, m_ref, l_ref, acc_ref, qsem, ksem = refs[24:]
    z, r = info_ref[0], info_ref[1]
    low = (z < 2).astype(jnp.int32)
    zx = jnp.where(z % 2 == 0, z + 1, z - 1)
    t_ids = (z, zx, jnp.where(low == 1, 2, 1), jnp.where(low == 1, 3, 0))

    def half_id(t, rr):
        return jnp.where(t < 2, 2 * rr + t, 2 * (7 - rr) + t - 2)

    r1 = jnp.where(r % 2 == 0, r + 1, r - 1)
    r2 = jnp.where(r < 2, r + 2, r - 2)
    r3 = 3 - r
    copies = [pltpu.make_async_copy(q_in[0].at[:, 2 * HD:], q_all.at[t_ids[0]], qsem.at[0])]
    inner = (z == 1) | (z == 2)
    for j in range(1, 4):

        @pl.when(inner)
        def _():
            pltpu.make_async_copy(q_in[j].at[:, 2 * HD:], q_all.at[t_ids[j]], qsem.at[j]).start()

        @pl.when(jnp.logical_not(inner))
        def _():
            pltpu.make_async_copy(q_shipped[j - 1], q_all.at[t_ids[j]], qsem.at[j]).start()

    for j in range(4):
        for k, rr in enumerate((r, r1, r2, r3)):
            copies.append(pltpu.make_async_copy(kv_in[4 * j + k], kv_all.at[half_id(t_ids[j], rr)], ksem.at[4 * j + k]))
    for c in copies:
        c.start()
    for c in copies:
        c.wait()
    for j in range(1, 4):
        pltpu.make_async_copy(q_shipped[j - 1], q_all.at[t_ids[j]], qsem.at[j]).wait()

    scale = LOG2E * HD ** -0.5
    rows = 2 * HB // NSUB

    def block(t, g, mode):
        k_blk = kv_all[g, :, 0:HD]
        v_blk = kv_all[g, :, HD:2 * HD]
        for sub in range(NSUB):
            head, off = divmod(sub * rows, HB)
            rs = pl.ds(sub * rows, rows)
            q_sub = q_all[t, pl.ds(off, rows), head * HD:(head + 1) * HD]
            s = lax.dot_general(q_sub, k_blk, (((1,), (1,)), ((), ())), preferred_element_type=jnp.float32)
            if mode != "full":
                row = lax.broadcasted_iota(jnp.int32, (rows, HB), 0) + off
                col = lax.broadcasted_iota(jnp.int32, (rows, HB), 1)
                keep = (col <= row) if mode == "diag" else (col > row)
                s = jnp.where(keep, s, -jnp.inf)
            m_cur = jnp.max(s, axis=1, keepdims=True)
            if mode == "diag":
                m_new = jnp.broadcast_to(m_cur, (rows, 128))
            else:
                m_old = m_ref[rs, :]
                m_new = jnp.maximum(m_old, m_cur)
                alpha = jnp.exp2((m_old - m_new) * scale)
            p = jnp.exp2((s - m_new[:, 0:1]) * scale)
            l_new = p[:, 0:128] + p[:, 128:256] + p[:, 256:384] + p[:, 384:512]
            pv = jnp.dot(p.astype(jnp.bfloat16), v_blk, preferred_element_type=jnp.float32)
            m_ref[rs, :] = m_new
            if mode == "diag":
                l_ref[rs, :] = l_new
                acc_ref[rs, :] = pv
            else:
                l_ref[rs, :] = l_ref[rs, :] * alpha + l_new
                acc_ref[rs, :] = acc_ref[rs, :] * jnp.concatenate([alpha, alpha], axis=1) + pv

    def one_piece(t, carry):
        g = half_id(t, r)
        block(t, g, "diag")

        def full_step(kb, c):
            block(t, kb, "full")
            return c

        lax.fori_loop(jnp.maximum(g - 7, 0), g, full_step, 0)

        @pl.when(g >= 8)
        def _():
            block(t, g - 8, "edge")

        for sub in range(NSUB):
            head, off = divmod(sub * rows, HB)
            rs = pl.ds(sub * rows, rows)
            total = jnp.sum(l_ref[rs, :], axis=1, keepdims=True)
            o_ref[t, pl.ds(off, rows), head * HD:(head + 1) * HD] = (acc_ref[rs, :] / total).astype(jnp.bfloat16)
        return carry

    lax.fori_loop(0, 4, one_piece, 0)


def attention(info, ps, qs, kvs):
    any_spec = pl.BlockSpec(memory_space=pl.ANY)
    return pl.pallas_call(
        attn_kernel,
        out_shape=jax.ShapeDtypeStruct((4, HB, 2 * HD), jnp.bfloat16),
        in_specs=[pl.BlockSpec(memory_space=pltpu.SMEM)] + [any_spec] * 23,
        out_specs=pl.BlockSpec(memory_space=pltpu.VMEM),
        scratch_shapes=[
            pltpu.VMEM((4, HB, 2 * HD), jnp.bfloat16),
            pltpu.VMEM((16, HB, 2 * HD), jnp.bfloat16),
            pltpu.VMEM((2 * HB, 128), jnp.float32),
            pltpu.VMEM((2 * HB, 128), jnp.float32),
            pltpu.VMEM((2 * HB, HD), jnp.float32),
            pltpu.SemaphoreType.DMA((4,)),
            pltpu.SemaphoreType.DMA((16,)),
        ],
        compiler_params=pltpu.CompilerParams(vmem_limit_bytes=48 * 1024 * 1024),
        cost_estimate=pl.CostEstimate(flops=17_000_000_000, bytes_accessed=12_000_000, transcendentals=16_000_000),
        name="window_attention",
    )(info, *ps, *qs, *kvs)


def out_kernel(info_ref, o0, o1, o2, o3, w0, w1, w2, w3, y_ref):
    total = jnp.dot(o0[...], w0[0], preferred_element_type=jnp.float32)
    for o_ref, w_ref in ((o1, w1), (o2, w2), (o3, w3)):
        total = total + jnp.dot(o_ref[...], w_ref[0], preferred_element_type=jnp.float32)
    y_ref[...] = total.astype(y_ref.dtype)


def out_project(info, pieces, w_full):
    d_model = w_full.shape[2]
    tile = 384
    piece_spec = pl.BlockSpec((HB, 2 * HD), lambda n, info: (0, 0))

    def w_spec(k):
        return pl.BlockSpec((1, 2 * HD, tile), lambda n, info: (info[2 + k], 0, n))

    return pl.pallas_call(
        out_kernel,
        out_shape=jax.ShapeDtypeStruct((HB, d_model), jnp.bfloat16),
        grid_spec=pltpu.PrefetchScalarGridSpec(
            num_scalar_prefetch=1,
            grid=(d_model // tile,),
            in_specs=[piece_spec] * 4 + [w_spec(k) for k in range(4)],
            out_specs=pl.BlockSpec((HB, tile), lambda n, info: (0, n)),
        ),
        compiler_params=pltpu.CompilerParams(vmem_limit_bytes=32 * 1024 * 1024),
        cost_estimate=pl.CostEstimate(flops=4_800_000_000, bytes_accessed=14_000_000, transcendentals=0),
        name="out_project",
    )(info, *pieces, w_full, w_full, w_full, w_full)


def solution(mesh):
    def sublayer(x, w_query, w_key, w_value, w_out):
        d_model = x.shape[1]
        z, r, dp = lax.axis_index("tp"), lax.axis_index("sp"), lax.axis_index("dp")
        inner = (z == 1) | (z == 2)
        n_part = mesh.shape["dp"] * mesh.shape["sp"]
        my_part = dp * mesh.shape["sp"] + r
        info = jnp.stack([z, r, z, z ^ 1, z ^ 2, z ^ 3]).astype(jnp.int32)

        def dot(a, b):
            return jnp.dot(a, b, preferred_element_type=jnp.float32).astype(jnp.bfloat16)

        from_edge = lax.ppermute(x, "tp", [(0, 1), (3, 2)])
        from_inner = lax.ppermute(x, "tp", [(1, 2), (2, 1)])
        from_far = lax.ppermute(from_edge, "tp", [(1, 2), (2, 1)])

        w_own = jnp.concatenate([w_key.reshape(d_model, HD), w_value.reshape(d_model, HD), w_query.reshape(d_model, 2 * HD)], axis=1)
        part = d_model // n_part
        w_part = lax.dynamic_slice_in_dim(w_own, my_part * part, part, 0)
        w_part = lax.ppermute(w_part, "tp", [(0, 1), (3, 2)])
        w_edge = lax.all_gather(w_part, ("dp", "sp"), axis=0, tiled=True)

        p_own = dot(x, w_own)
        p_b_in = dot(from_edge, w_own)
        p_c_in = dot(from_inner, w_own)
        p_d_in = dot(from_far, w_own)
        kv_own = p_own[:, :2 * HD]

        def ship(src, mine):
            made = dot(src, w_edge)
            kv = lax.ppermute(made[:, :2 * HD], "tp", [(1, 0), (2, 3)])
            q = lax.ppermute(made[:, 2 * HD:], "tp", [(1, 0), (2, 3)])
            return jnp.where(inner, mine[:, :2 * HD], kv), q

        kv_b, q_b = ship(x, p_b_in)
        kv_c, q_c = ship(from_inner, p_c_in)
        kv_d, q_d = ship(from_far, p_d_in)

        def spread(kv):
            across = lax.ppermute(kv, "sp", [(0, 2), (1, 3), (2, 0), (3, 1)])
            mate = lax.ppermute(kv, "sp", [(0, 1), (1, 0), (2, 3), (3, 2)])
            mate_across = lax.ppermute(across, "sp", [(0, 1), (1, 0), (2, 3), (3, 2)])
            return kv, mate, across, mate_across

        kvs = spread(kv_own) + spread(kv_b) + spread(kv_c) + spread(kv_d)
        o = attention(info, (p_own, p_b_in, p_c_in, p_d_in), (q_b, q_c, q_d), kvs)

        wo_rows = w_out.reshape(2 * HD, d_model)
        wo_part = lax.dynamic_slice_in_dim(wo_rows, my_part * (2 * HD // n_part), 2 * HD // n_part, 0)
        wo_full = lax.all_gather(wo_part, ("tp", "dp", "sp"), axis=0, tiled=True).reshape(4, 2 * HD, d_model)

        def o_for(k):
            return lax.dynamic_index_in_dim(o, z ^ k, 0, keepdims=False)

        pieces = [o_for(0)]
        for k in range(1, 4):
            pieces.append(lax.ppermute(o_for(k), "tp", [(i, i ^ k) for i in range(4)]))
        return out_project(info, pieces, wo_full)

    return jax.shard_map(sublayer, mesh=mesh, in_specs=(P(("dp", "sp", "tp"), None), P(None, "tp", None), P(None, "tp", None), P(None, "tp", None), P("tp", None, None)), out_specs=P(("dp", "sp", "tp"), None), check_vma=False)
```

time: 775 us -> 409 us (0.53)
  the two profiles are of different devices: /device:TPU:26 before, /device:TPU:13 now
where the time goes in v1:
time: 409 us
  waiting for transfers between devices  230 us (56%)
  Pallas kernels  61.1 us (15%)
  starting transfers between devices  42.6 us (10%)
  matrix products  37.3 us (9%)
  local copies, waits for them, and re-layouts  20.4 us (5%)
  between operations  13.7 us (3%)
    ppermute x1, waiting for transfers between devices, sublayer(): from_far = lax.ppermute(from_edge, 'tp', [(1, 2), (2, 1)])  79.6 us
    pallas_call x1, Pallas kernels, attention(): pl.pallas_call(attn_kernel, out_shape=jax.ShapeDtypeStruct((4, HB, 2 * HD...  51 us
    ppermute x1, waiting for transfers between devices, sublayer(): from_edge = lax.ppermute(x, 'tp', [(0, 1), (3, 2)])  42.3 us
    ppermute x3, waiting for transfers between devices, sublayer(): pieces.append(lax.ppermute(o_for(k), 'tp', [(i, i ^ k) for i in range(4)]))  40.6 us
    dot_general x7, matrix products, dot(): jnp.dot(a, b, preferred_element_type=jnp.float32).astype(jnp.bfloat16)  37.3 us
    ppermute x3, waiting for transfers between devices, ship(): kv = lax.ppermute(made[:, :2 * HD], 'tp', [(1, 0), (2, 3)])  22.6 us
    unnamed x43, local copies, waits for them, and re-layouts  17.6 us
    ppermute x4, waiting for transfers between devices, spread(): across = lax.ppermute(kv, 'sp', [(0, 2), (1, 3), (2, 0), (3, 1)])  17 us
  transfers between devices with their start and end apart: 27, of which 14 were waited for; matrix products, arithmetic and copies ran while one was open for 10% of the time, Pallas kernels for 12%

profile of v1, /device:TPU:13, one launch (start us, length us, event | category | flops | bytes accessed | tf_op | source)
XLA Modules:
  0.0 408.6 jit_solution(15742395801839194289)
XLA Ops:
  6.5 3.6 copy.20
  10.2 2.3 pad_maximum_fusion
  12.5 1.3 collective-permute-start.3
  13.8 14.9 %collective-permute-done.3 = bf16[288,1024]{1,0:T(8,128)(2,1)} collective-permute-done((bf16[288,1024]{1,0:T(8,128)(2,1)S(1)}, bf16[288,1024]{1,0:T(8,128)(2,1)}, u32[]{:S(2)}, u32[]{:S(2)}) %collective-permute-start.3) | collective-permute-done | bytes 589856 | tf_op jit(solution)/shard_map/ppermute | solution.py:183
  28.8 0.8 constant_dynamic-slice_fusion
  29.6 1.3 collective-permute-start
  30.9 3.2 collective-permute-start.1
  34.1 5.3 %fusion.refs_0_ = bf16[512,1024]{1,0:T(8,128)(2,1)S(1)} fusion(bf16[512,2304]{1,0:T(8,128)(2,1)} %param.5, bf16[2304,512]{1,0:T(8,128)(2,1)} %bitcast.49, bf16[2304,256]{1,0:T(8,128)(2,1)S(1)} %bitcast.55, bf16[2304,256]{1,0:T(8,128)(2,1)} %bitcast.60), kind=kOutput, calls=%fused_computation.8 | convolution fusion | flops 2430599168 | bytes 8126464 | tf_op jit(solution)/shard_map/dot_general | solution.py:174
  39.4 1.0 copy-done.16
  40.4 0.3 collective-permute-start.8
  40.7 42.3 %collective-permute-done = bf16[512,2304]{1,0:T(8,128)(2,1)} collective-permute-done((bf16[512,2304]{1,0:T(8,128)(2,1)}, bf16[512,2304]{1,0:T(8,128)(2,1)}, u32[]{:S(2)}, u32[]{:S(2)}) %collective-permute-start) | collective-permute-done | bytes 2359328 | tf_op jit(solution)/shard_map/ppermute | solution.py:176
  83.1 3.2 collective-permute-start.2
  86.3 2.7 collective-permute-start.7
  89.0 0.1 collective-permute-start.9
  89.1 6.4 %fusion.1.refs_1_ = bf16[512,1024]{1,0:T(8,128)(2,1)} fusion(bf16[512,2304]{1,0:T(8,128)(2,1)} %collective-permute-done, bf16[2304,512]{1,0:T(8,128)(2,1)} %bitcast.50, bf16[2304,256]{1,0:T(8,128)(2,1)S(1)} %bitcast.56, bf16[2304,256]{1,0:T(8,128)(2,1)} %bitcast.61), kind=kOutput, calls=%fused_computation.9 | convolution fusion | flops 2430599168 | bytes 8126464 | tf_op jit(solution)/shard_map/dot_general | solution.py:174
  95.6 5.6 %fusion.2.refs_2_ = bf16[512,1024]{1,0:T(8,128)(2,1)} fusion(bf16[512,2304]{1,0:T(8,128)(2,1)} %collective-permute-done.1, bf16[2304,512]{1,0:T(8,128)(2,1)S(1)} %bitcast.51, bf16[2304,256]{1,0:T(8,128)(2,1)S(1)} %bitcast.57, bf16[2304,256]{1,0:T(8,128)(2,1)S(1)} %bitcast.62), kind=kOutput, calls=%fused_computation.10 | convolution fusion | flops 2430599168 | bytes 8126464 | tf_op jit(solution)/shard_map/dot_general | solution.py:174
  101.2 79.6 %collective-permute-done.2 = bf16[512,2304]{1,0:T(8,128)(2,1)} collective-permute-done((bf16[512,2304]{1,0:T(8,128)(2,1)}, bf16[512,2304]{1,0:T(8,128)(2,1)}, u32[]{:S(2)}, u32[]{:S(2)}) %collective-permute-start.2) | collective-permute-done | bytes 2359328 | tf_op jit(solution)/shard_map/ppermute | solution.py:178
  180.8 5.5 %fusion.3.refs_3_ = bf16[512,1024]{1,0:T(8,128)(2,1)} fusion(bf16[512,2304]{1,0:T(8,128)(2,1)} %collective-permute-done.2, bf16[2304,512]{1,0:T(8,128)(2,1)S(1)} %bitcast.52, bf16[2304,256]{1,0:T(8,128)(2,1)S(1)} %bitcast.58, bf16[2304,256]{1,0:T(8,128)(2,1)S(1)} %bitcast.63), kind=kOutput, calls=%fused_computation.11 | convolution fusion | flops 2430599168 | bytes 8126464 | tf_op jit(solution)/shard_map/dot_general | solution.py:174
  186.3 5.8 %fusion.4 = bf16[512,1024]{1,0:T(8,128)(2,1)S(1)} fusion(bf16[512,2304]{1,0:T(8,128)(2,1)} %param.5, bf16[2304,1024]{1,0:T(8,128)(2,1)} %all-gather.3.cloned.1.call-done), kind=kOutput, calls=%fused_computation.12 | convolution fusion | flops 2416443392 | bytes 8126464 | tf_op jit(solution)/shard_map/dot_general | solution.py:174
  192.2 1.3 collective-permute-start.4
  193.5 1.3 collective-permute-start.10
  194.9 4.3 %fusion.5 = bf16[512,1024]{1,0:T(8,128)(2,1)S(1)} fusion(bf16[512,2304]{1,0:T(8,128)(2,1)} %collective-permute-done.1, bf16[2304,1024]{1,0:T(8,128)(2,1)S(1)} %copy-done.20), kind=kOutput, calls=%fused_computation.13 | convolution fusion | flops 2416443392 | bytes 8126464 | tf_op jit(solution)/shard_map/dot_general | solution.py:174
  199.3 1.5 collective-permute-start.14
  200.8 4.3 %fusion.6 = bf16[512,1024]{1,0:T(8,128)(2,1)S(1)} fusion(bf16[512,2304]{1,0:T(8,128)(2,1)} %collective-permute-done.2, bf16[2304,1024]{1,0:T(8,128)(2,1)S(1)} %copy-done.20), kind=kOutput, calls=%fused_computation.14 | convolution fusion | flops 2416443392 | bytes 8126464 | tf_op jit(solution)/shard_map/dot_general | solution.py:174
  205.2 9.4 %collective-permute-done.10 = bf16[512,512]{1,0:T(8,128)(2,1)S(1)} collective-permute-done((bf16[512,512]{1,0:T(8,128)(2,1)S(1)}, bf16[512,512]{1,0:T(8,128)(2,1)S(1)}, u32[]{:S(2)}, u32[]{:S(2)}) %collective-permute-start.10) | collective-permute-done | bytes 524320 | tf_op jit(solution)/shard_map/ppermute | solution.py:194
  214.6 4.1 %collective-permute-start.18 = (bf16[512,512]{1,0:T(8,128)(2,1)S(1)}, bf16[512,512]{1,0:T(8,128)(2,1)S(1)}, u32[]{:S(2)}, u32[]{:S(2)}) collective-permute-start(bf16[512,512]{1,0:T(8,128)(2,1)S(1)} %get-tuple-element.9), channel_id=1, source_target_pairs={{4,0},{8,12},{5,1},{9,13},{6,2},{10,14},{7,3},{11,15},{20,16},{24,... | collective-permute-start | bytes 1572872 | tf_op jit(solution)/shard_map/ppermute | solution.py:194
  218.9 7.0 %collective-permute-done.14 = bf16[512,512]{1,0:T(8,128)(2,1)S(1)} collective-permute-done((bf16[512,512]{1,0:T(8,128)(2,1)S(1)}, bf16[512,512]{1,0:T(8,128)(2,1)S(1)}, u32[]{:S(2)}, u32[]{:S(2)}) %collective-permute-start.14) | collective-permute-done | bytes 524320 | tf_op jit(solution)/shard_map/ppermute | solution.py:194
  225.9 4.1 %collective-permute-start.5 = (bf16[512,512]{1,0:T(8,128)(2,1)S(1)}, bf16[512,512]{1,0:T(8,128)(2,1)S(1)}, u32[]{:S(2)}, u32[]{:S(2)}) collective-permute-start(bf16[512,512]{1,0:T(8,128)(2,1)S(1)} %get-tuple-element.12), channel_id=1, source_target_pairs={{4,0},{8,12},{5,1},{9,13},{6,2},{10,14},{7,3},{11,15},{20,16},{24,... | collective-permute-start | bytes 1572872 | tf_op jit(solution)/shard_map/ppermute | solution.py:195
  230.0 0.9 slice_select_fusion.1.refs_15_
  230.9 6.2 %collective-permute-done.18 = bf16[512,512]{1,0:T(8,128)(2,1)S(1)} collective-permute-done((bf16[512,512]{1,0:T(8,128)(2,1)S(1)}, bf16[512,512]{1,0:T(8,128)(2,1)S(1)}, u32[]{:S(2)}, u32[]{:S(2)}) %collective-permute-start.18) | collective-permute-done | bytes 524320 | tf_op jit(solution)/shard_map/ppermute | solution.py:194
  237.1 4.1 %collective-permute-start.6 = (bf16[512,512]{1,0:T(8,128)(2,1)S(1)}, bf16[512,512]{1,0:T(8,128)(2,1)S(1)}, u32[]{:S(2)}, u32[]{:S(2)}) collective-permute-start(bf16[512,512]{1,0:T(8,128)(2,1)S(1)} %get-tuple-element.10), channel_id=1, source_target_pairs={{4,0},{8,12},{5,1},{9,13},{6,2},{10,14},{7,3},{11,15},{20,16},{24,... | collective-permute-start | bytes 1572872 | tf_op jit(solution)/shard_map/ppermute | solution.py:195
  241.3 0.9 slice_select_fusion.refs_19_
  242.1 4.3 %collective-permute-start.11 = (bf16[512,512]{1,0:T(8,128)(2,1)S(1)}, bf16[512,512]{1,0:T(8,128)(2,1)S(1)}, u32[]{:S(2)}, u32[]{:S(2)}) collective-permute-start(bf16[512,512]{1,0:T(8,128)(2,1)S(1)} %slice_select_fusion.2.refs_11_), channel_id=1, source_target_pairs={{0,1},{1,0},{2,3},{3,2},{4,5},{5,4},{6,7},{7,6},{8,9},{9,8},{10,11... | collective-permute-start | bytes 1572872 | tf_op jit(solution)/shard_map/ppermute | solution.py:204
  246.4 0.3 collective-permute-start.12
  246.7 1.2 collective-permute-start.16
  247.9 0.5 collective-permute-done.5.refs_5_
  248.4 0.8 copy-done.7
  249.1 0.3 collective-permute-start.20
  249.5 10.1 %collective-permute-done.6.refs_6_ = bf16[512,512]{1,0:T(8,128)(2,1)S(1)} collective-permute-done((bf16[512,512]{1,0:T(8,128)(2,1)S(1)}, bf16[512,512]{1,0:T(8,128)(2,1)S(1)}, u32[]{:S(2)}, u32[]{:S(2)}) %collective-permute-start.6) | collective-permute-done | bytes 524320 | tf_op jit(solution)/shard_map/ppermute | solution.py:195
  259.6 0.8 copy-done.9
  260.4 2.2 collective-permute-start.15
  262.6 0.8 copy-done.11
  263.4 0.5 collective-permute-start.13
  263.9 7.2 %collective-permute-done.16.refs_17_ = bf16[512,512]{1,0:T(8,128)(2,1)} collective-permute-done((bf16[512,512]{1,0:T(8,128)(2,1)}, bf16[512,512]{1,0:T(8,128)(2,1)}, u32[]{:S(2)}, u32[]{:S(2)}) %collective-permute-start.16) | collective-permute-done | bytes 524320 | tf_op jit(solution)/shard_map/ppermute | solution.py:203
  271.1 1.5 collective-permute-start.17
  272.6 9.8 %collective-permute-done.20.refs_21_ = bf16[512,512]{1,0:T(8,128)(2,1)} collective-permute-done((bf16[512,512]{1,0:T(8,128)(2,1)}, bf16[512,512]{1,0:T(8,128)(2,1)}, u32[]{:S(2)}, u32[]{:S(2)}) %collective-permute-start.20) | collective-permute-done | bytes 524320 | tf_op jit(solution)/shard_map/ppermute | solution.py:203
  282.4 0.9 collective-permute-start.21
  283.4 1.8 collective-permute-done.21.refs_22_
  285.2 1.0 copy-done.8
  286.2 1.0 copy-done.10
  287.3 1.0 copy-done.12
  288.3 51.0 %window_attention.1 = bf16[4,512,512]{2,1,0:T(8,128)(2,1)} custom-call(s32[6]{0:T(128)S(1)} %stack.24.info_ref, bf16[512,1024]{1,0:T(8,128)(2,1)} %copy-done.16, bf16[512,1024]{1,0:T(8,128)(2,1)} %fusion.1.refs_1_, bf16[512,1024]{1,0:T(8,128)(2,1)} %fusion.2.refs_2_, bf16[512,1024]{1,0:T(8,128)(2,1)} %fusion.3.refs_3_, ...), custom_call_target="tpu_custom_call" | custom-call | flops 16999999488 | bytes 12000000 | tf_op jit(solution)/shard_map/window_attention/pallas_call | solution.py:114
  339.4 1.7 dynamic-slice_bitcast_fusion
  341.1 1.6 collective-permute-start.23
  342.7 1.0 collective-permute-start.24
  343.7 12.4 %collective-permute-done.22.o1 = bf16[512,512]{1,0:T(8,128)(2,1)S(1)} collective-permute-done((bf16[512,512]{1,0:T(8,128)(2,1)S(1)}, bf16[512,512]{1,0:T(8,128)(2,1)S(1)}, u32[]{:S(2)}, u32[]{:S(2)}) %collective-permute-start.22) | collective-permute-done | bytes 524320 | tf_op jit(solution)/shard_map/ppermute | solution.py:220
  356.1 20.8 %collective-permute-done.23.o2 = bf16[512,512]{1,0:T(8,128)(2,1)S(1)} collective-permute-done((bf16[512,512]{1,0:T(8,128)(2,1)S(1)}, bf16[512,512]{1,0:T(8,128)(2,1)S(1)}, u32[]{:S(2)}, u32[]{:S(2)}) %collective-permute-start.23) | collective-permute-done | bytes 524320 | tf_op jit(solution)/shard_map/ppermute | solution.py:220
  376.9 0.8 copy-done.3
  377.7 7.4 %collective-permute-done.24.o3 = bf16[512,512]{1,0:T(8,128)(2,1)S(1)} collective-permute-done((bf16[512,512]{1,0:T(8,128)(2,1)S(1)}, bf16[512,512]{1,0:T(8,128)(2,1)S(1)}, u32[]{:S(2)}, u32[]{:S(2)}) %collective-permute-start.24) | collective-permute-done | bytes 524320 | tf_op jit(solution)/shard_map/ppermute | solution.py:220
  385.1 0.8 copy-done.5
  386.0 3.7 copy-done.2
  389.7 1.0 copy-done.4
  390.7 1.0 copy-done.6
  391.7 10.0 %out_project.1 = bf16[512,2304]{1,0:T(8,128)(2,1)} custom-call(s32[6]{0:T(128)S(1)} %stack.24.info_ref, bf16[512,512]{1,0:T(8,128)(2,1)S(1)} %get-tuple-element.8.o0, bf16[512,512]{1,0:T(8,128)(2,1)S(1)} %collective-permute-done.22.o1, bf16[512,512]{1,0:T(8,128)(2,1)S(1)} %copy-done.4, bf16[512,512]{1,0:T(8,128)(2,1)S(1)} %copy-done.6, ...), custom_call_target="tpu_custom_call" | custom-call | flops 4800000000 | bytes 14000000 | tf_op jit(solution)/shard_map/out_project/pallas_call | solution.py:149
  (56 shorter events, 0.7 us)
Async XLA Ops:
  6.5 22.2 %copy-start = (bf16[2,256,2304]{2,1,0:T(8,128)(2,1)S(1)}, bf16[2,256,2304]{2,1,0:T(8,128)(2,1)}, u32[]{:S(2)}) copy-start(bf16[2,256,2304]{2,1,0:T(8,128)(2,1)} %param.9) | copy-start | bytes 7077892
  6.5 179.8 %all-gather.3.cloned.1.call-start = ((), (), s32[]{:S(2)}) async-start(), calls=%async_computation | async-start | bytes 5308416 | tf_op jit(solution)/shard_map/all_gather | solution.py:184
  6.5 3.6 copy-start.14
  12.5 16.2 %collective-permute-start.3 = (bf16[288,1024]{1,0:T(8,128)(2,1)S(1)}, bf16[288,1024]{1,0:T(8,128)(2,1)}, u32[]{:S(2)}, u32[]{:S(2)}) collective-permute-start(bf16[288,1024]{1,0:T(8,128)(2,1)S(1)} %constant_dynamic-slice_fusion.1), channel_id=1, source_target_pairs={{0,4},{12,8},{1,5},{13,9},{2,6},{14,10},{3,7},{15,11},{16,20},{28,... | collective-permute-start | bytes 1769480 | tf_op jit(solution)/shard_map/ppermute | solution.py:183
  28.7 357.2 %all-gather.5.cloned.1.call-start = ((), (), s32[]{:S(2)}) async-start(), calls=%async_computation.1 | async-start | bytes 9732096 | tf_op jit(solution)/shard_map/all_gather | solution.py:213
  29.6 53.5 %collective-permute-start = (bf16[512,2304]{1,0:T(8,128)(2,1)}, bf16[512,2304]{1,0:T(8,128)(2,1)}, u32[]{:S(2)}, u32[]{:S(2)}) collective-permute-start(bf16[512,2304]{1,0:T(8,128)(2,1)} %param.5), channel_id=1, source_target_pairs={{0,4},{12,8},{1,5},{13,9},{2,6},{14,10},{3,7},{15,11},{16,20},{28,... | collective-permute-start | bytes 7077896 | tf_op jit(solution)/shard_map/ppermute | solution.py:176
  30.9 64.7 %collective-permute-start.1 = (bf16[512,2304]{1,0:T(8,128)(2,1)}, bf16[512,2304]{1,0:T(8,128)(2,1)}, u32[]{:S(2)}, u32[]{:S(2)}) collective-permute-start(bf16[512,2304]{1,0:T(8,128)(2,1)} %param.5), channel_id=1, source_target_pairs={{4,8},{8,4},{5,9},{9,5},{6,10},{10,6},{7,11},{11,7},{20,24},{24,20... | collective-permute-start | bytes 7077896 | tf_op jit(solution)/shard_map/ppermute | solution.py:177
  39.4 1.0 copy-start.16
  40.4 48.6 %collective-permute-start.8 = (bf16[512,512]{1,0:T(8,128)(2,1)S(1)}, bf16[512,512]{1,0:T(8,128)(2,1)S(1)}, u32[]{:S(2)}, u32[]{:S(2)}) collective-permute-start(bf16[512,512]{1,0:T(8,128)(2,1)S(1)} %slice.43.refs_7_), channel_id=1, source_target_pairs={{0,2},{1,3},{2,0},{3,1},{4,6},{5,7},{6,4},{7,5},{8,10},{9,11},{10,... | collective-permute-start | bytes 1572872 | tf_op jit(solution)/shard_map/ppermute | solution.py:203
  83.1 97.7 %collective-permute-start.2 = (bf16[512,2304]{1,0:T(8,128)(2,1)}, bf16[512,2304]{1,0:T(8,128)(2,1)}, u32[]{:S(2)}, u32[]{:S(2)}) collective-permute-start(bf16[512,2304]{1,0:T(8,128)(2,1)} %collective-permute-done), channel_id=1, source_target_pairs={{4,8},{8,4},{5,9},{9,5},{6,10},{10,6},{7,11},{11,7},{20,24},{24,20... | collective-permute-start | bytes 7077896 | tf_op jit(solution)/shard_map/ppermute | solution.py:178
  86.3 155.9 %collective-permute-start.7 = (bf16[512,512]{1,0:T(8,128)(2,1)S(1)}, bf16[512,512]{1,0:T(8,128)(2,1)S(1)}, u32[]{:S(2)}, u32[]{:S(2)}) collective-permute-start(bf16[512,512]{1,0:T(8,128)(2,1)S(1)} %slice.43.refs_7_), channel_id=1, source_target_pairs={{0,1},{1,0},{2,3},{3,2},{4,5},{5,4},{6,7},{7,6},{8,9},{9,8},{10,11... | collective-permute-start | bytes 1572872 | tf_op jit(solution)/shard_map/ppermute | solution.py:204
  89.0 6.6 %copy-start.13 = (bf16[288,8,2,256]{3,1,2,0:T(8,128)(2,1)S(1)}, bf16[288,8,2,256]{3,1,2,0:T(8,128)(2,1)}, u32[]{:S(2)}) copy-start(bf16[288,8,2,256]{3,1,2,0:T(8,128)(2,1)} %copy.20) | copy-start | bytes 7077892
  89.0 6.6 %copy-start.15 = (bf16[2304,1,256]{2,0,1:T(8,128)(2,1)S(1)}, bf16[2304,1,256]{2,0,1:T(8,128)(2,1)}, u32[]{:S(2)}) copy-start(bf16[2304,1,256]{2,0,1:T(8,128)(2,1)} %param.7) | copy-start | bytes 3538948
  89.0 157.4 %collective-permute-start.9 = (bf16[512,512]{1,0:T(8,128)(2,1)S(1)}, bf16[512,512]{1,0:T(8,128)(2,1)S(1)}, u32[]{:S(2)}, u32[]{:S(2)}) collective-permute-start(bf16[512,512]{1,0:T(8,128)(2,1)S(1)} %collective-permute-done.8.refs_9_), channel_id=1, source_target_pairs={{0,1},{1,0},{2,3},{3,2},{4,5},{5,4},{6,7},{7,6},{8,9},{9,8},{10,11... | collective-permute-start | bytes 1572872 | tf_op jit(solution)/shard_map/ppermute | solution.py:205
  186.3 8.6 %copy-start.20 = (bf16[2304,1024]{1,0:T(8,128)(2,1)S(1)}, bf16[2304,1024]{1,0:T(8,128)(2,1)}, u32[]{:S(2)}) copy-start(bf16[2304,1024]{1,0:T(8,128)(2,1)} %all-gather.3.cloned.1.call-done) | copy-start | bytes 14155780
  192.2 54.5 %collective-permute-start.4 = (bf16[512,512]{1,0:T(8,128)(2,1)S(1)}, bf16[512,512]{1,0:T(8,128)(2,1)S(1)}, u32[]{:S(2)}, u32[]{:S(2)}) collective-permute-start(bf16[512,512]{1,0:T(8,128)(2,1)S(1)} %get-tuple-element.14), channel_id=1, source_target_pairs={{4,0},{8,12},{5,1},{9,13},{6,2},{10,14},{7,3},{11,15},{20,16},{24,... | collective-permute-start | bytes 1572872 | tf_op jit(solution)/shard_map/ppermute | solution.py:195
  193.5 21.1 %collective-permute-start.10 = (bf16[512,512]{1,0:T(8,128)(2,1)S(1)}, bf16[512,512]{1,0:T(8,128)(2,1)S(1)}, u32[]{:S(2)}, u32[]{:S(2)}) collective-permute-start(bf16[512,512]{1,0:T(8,128)(2,1)S(1)} %get-tuple-element.13), channel_id=1, source_target_pairs={{4,0},{8,12},{5,1},{9,13},{6,2},{10,14},{7,3},{11,15},{20,16},{24,... | collective-permute-start | bytes 1572872 | tf_op jit(solution)/shard_map/ppermute | solution.py:194
  199.3 26.6 %collective-permute-start.14 = (bf16[512,512]{1,0:T(8,128)(2,1)S(1)}, bf16[512,512]{1,0:T(8,128)(2,1)S(1)}, u32[]{:S(2)}, u32[]{:S(2)}) collective-permute-start(bf16[512,512]{1,0:T(8,128)(2,1)S(1)} %get-tuple-element.11), channel_id=1, source_target_pairs={{4,0},{8,12},{5,1},{9,13},{6,2},{10,14},{7,3},{11,15},{20,16},{24,... | collective-permute-start | bytes 1572872 | tf_op jit(solution)/shard_map/ppermute | solution.py:194
  205.1 13.7 %copy-start.17 = (bf16[512,1024]{1,0:T(8,128)(2,1)S(1)}, bf16[512,1024]{1,0:T(8,128)(2,1)}, u32[]{:S(2)}) copy-start(bf16[512,1024]{1,0:T(8,128)(2,1)} %fusion.1.refs_1_) | copy-start | bytes 3145732
  205.1 24.9 %copy-start.18 = (bf16[512,1024]{1,0:T(8,128)(2,1)S(1)}, bf16[512,1024]{1,0:T(8,128)(2,1)}, u32[]{:S(2)}) copy-start(bf16[512,1024]{1,0:T(8,128)(2,1)} %fusion.2.refs_2_) | copy-start | bytes 3145732
  205.2 36.1 %copy-start.19 = (bf16[512,1024]{1,0:T(8,128)(2,1)S(1)}, bf16[512,1024]{1,0:T(8,128)(2,1)}, u32[]{:S(2)}) copy-start(bf16[512,1024]{1,0:T(8,128)(2,1)} %fusion.3.refs_3_) | copy-start | bytes 3145732
  214.6 22.5 %collective-permute-start.18 = (bf16[512,512]{1,0:T(8,128)(2,1)S(1)}, bf16[512,512]{1,0:T(8,128)(2,1)S(1)}, u32[]{:S(2)}, u32[]{:S(2)}) collective-permute-start(bf16[512,512]{1,0:T(8,128)(2,1)S(1)} %get-tuple-element.9), channel_id=1, source_target_pairs={{4,0},{8,12},{5,1},{9,13},{6,2},{10,14},{7,3},{11,15},{20,16},{24,... | collective-permute-start | bytes 1572872 | tf_op jit(solution)/shard_map/ppermute | solution.py:194
  225.9 22.5 %collective-permute-start.5 = (bf16[512,512]{1,0:T(8,128)(2,1)S(1)}, bf16[512,512]{1,0:T(8,128)(2,1)S(1)}, u32[]{:S(2)}, u32[]{:S(2)}) collective-permute-start(bf16[512,512]{1,0:T(8,128)(2,1)S(1)} %get-tuple-element.12), channel_id=1, source_target_pairs={{4,0},{8,12},{5,1},{9,13},{6,2},{10,14},{7,3},{11,15},{20,16},{24,... | collective-permute-start | bytes 1572872 | tf_op jit(solution)/shard_map/ppermute | solution.py:195
  237.1 22.5 %collective-permute-start.6 = (bf16[512,512]{1,0:T(8,128)(2,1)S(1)}, bf16[512,512]{1,0:T(8,128)(2,1)S(1)}, u32[]{:S(2)}, u32[]{:S(2)}) collective-permute-start(bf16[512,512]{1,0:T(8,128)(2,1)S(1)} %get-tuple-element.10), channel_id=1, source_target_pairs={{4,0},{8,12},{5,1},{9,13},{6,2},{10,14},{7,3},{11,15},{20,16},{24,... | collective-permute-start | bytes 1572872 | tf_op jit(solution)/shard_map/ppermute | solution.py:195
  242.1 20.5 %collective-permute-start.11 = (bf16[512,512]{1,0:T(8,128)(2,1)S(1)}, bf16[512,512]{1,0:T(8,128)(2,1)S(1)}, u32[]{:S(2)}, u32[]{:S(2)}) collective-permute-start(bf16[512,512]{1,0:T(8,128)(2,1)S(1)} %slice_select_fusion.2.refs_11_), channel_id=1, source_target_pairs={{0,1},{1,0},{2,3},{3,2},{4,5},{5,4},{6,7},{7,6},{8,9},{9,8},{10,11... | collective-permute-start | bytes 1572872 | tf_op jit(solution)/shard_map/ppermute | solution.py:204
  246.4 17.0 %collective-permute-start.12 = (bf16[512,512]{1,0:T(8,128)(2,1)S(1)}, bf16[512,512]{1,0:T(8,128)(2,1)}, u32[]{:S(2)}, u32[]{:S(2)}) collective-permute-start(bf16[512,512]{1,0:T(8,128)(2,1)S(1)} %slice_select_fusion.2.refs_11_), channel_id=1, source_target_pairs={{0,2},{1,3},{2,0},{3,1},{4,6},{5,7},{6,4},{7,5},{8,10},{9,11},{10,... | collective-permute-start | bytes 1572872 | tf_op jit(solution)/shard_map/ppermute | solution.py:203
  246.7 24.5 %collective-permute-start.16 = (bf16[512,512]{1,0:T(8,128)(2,1)}, bf16[512,512]{1,0:T(8,128)(2,1)}, u32[]{:S(2)}, u32[]{:S(2)}) collective-permute-start(bf16[512,512]{1,0:T(8,128)(2,1)} %slice_select_fusion.1.refs_15_), channel_id=1, source_target_pairs={{0,2},{1,3},{2,0},{3,1},{4,6},{5,7},{6,4},{7,5},{8,10},{9,11},{10,... | collective-permute-start | bytes 1572872 | tf_op jit(solution)/shard_map/ppermute | solution.py:203
  248.4 0.8 copy-start.7
  249.1 33.2 %collective-permute-start.20 = (bf16[512,512]{1,0:T(8,128)(2,1)}, bf16[512,512]{1,0:T(8,128)(2,1)}, u32[]{:S(2)}, u32[]{:S(2)}) collective-permute-start(bf16[512,512]{1,0:T(8,128)(2,1)} %slice_select_fusion.refs_19_), channel_id=1, source_target_pairs={{0,2},{1,3},{2,0},{3,1},{4,6},{5,7},{6,4},{7,5},{8,10},{9,11},{10,... | collective-permute-start | bytes 1572872 | tf_op jit(solution)/shard_map/ppermute | solution.py:203
  259.6 0.8 copy-start.9
  260.4 23.0 %collective-permute-start.15 = (bf16[512,512]{1,0:T(8,128)(2,1)}, bf16[512,512]{1,0:T(8,128)(2,1)}, u32[]{:S(2)}, u32[]{:S(2)}) collective-permute-start(bf16[512,512]{1,0:T(8,128)(2,1)} %slice_select_fusion.1.refs_15_), channel_id=1, source_target_pairs={{0,1},{1,0},{2,3},{3,2},{4,5},{5,4},{6,7},{7,6},{8,9},{9,8},{10,11... | collective-permute-start | bytes 1572872 | tf_op jit(solution)/shard_map/ppermute | solution.py:204
  262.6 0.8 copy-start.11
  263.4 20.0 %collective-permute-start.19 = (bf16[512,512]{1,0:T(8,128)(2,1)}, bf16[512,512]{1,0:T(8,128)(2,1)}, u32[]{:S(2)}, u32[]{:S(2)}) collective-permute-start(bf16[512,512]{1,0:T(8,128)(2,1)} %slice_select_fusion.refs_19_), channel_id=1, source_target_pairs={{0,1},{1,0},{2,3},{3,2},{4,5},{5,4},{6,7},{7,6},{8,9},{9,8},{10,11... | collective-permute-start | bytes 1572872 | tf_op jit(solution)/shard_map/ppermute | solution.py:204
  263.4 20.0 %collective-permute-start.13 = (bf16[512,512]{1,0:T(8,128)(2,1)}, bf16[512,512]{1,0:T(8,128)(2,1)}, u32[]{:S(2)}, u32[]{:S(2)}) collective-permute-start(bf16[512,512]{1,0:T(8,128)(2,1)} %collective-permute-done.12.refs_13_), channel_id=1, source_target_pairs={{0,1},{1,0},{2,3},{3,2},{4,5},{5,4},{6,7},{7,6},{8,9},{9,8},{10,11... | collective-permute-start | bytes 1572872 | tf_op jit(solution)/shard_map/ppermute | solution.py:205
  271.1 12.3 %collective-permute-start.17 = (bf16[512,512]{1,0:T(8,128)(2,1)}, bf16[512,512]{1,0:T(8,128)(2,1)}, u32[]{:S(2)}, u32[]{:S(2)}) collective-permute-start(bf16[512,512]{1,0:T(8,128)(2,1)} %collective-permute-done.16.refs_17_), channel_id=1, source_target_pairs={{0,1},{1,0},{2,3},{3,2},{4,5},{5,4},{6,7},{7,6},{8,9},{9,8},{10,11... | collective-permute-start | bytes 1572872 | tf_op jit(solution)/shard_map/ppermute | solution.py:205
  282.4 2.8 collective-permute-start.21
  285.2 1.0 copy-start.8
  286.2 1.0 copy-start.10
  287.3 1.0 copy-start.12
  341.0 15.1 %collective-permute-start.22 = (bf16[512,512]{1,0:T(8,128)(2,1)S(1)}, bf16[512,512]{1,0:T(8,128)(2,1)S(1)}, u32[]{:S(2)}, u32[]{:S(2)}) collective-permute-start(bf16[512,512]{1,0:T(8,128)(2,1)S(1)} %get-tuple-element.7), channel_id=1, source_target_pairs={{0,4},{4,0},{8,12},{12,8},{1,5},{5,1},{9,13},{13,9},{2,6},{6,2},{1... | collective-permute-start | bytes 1572872 | tf_op jit(solution)/shard_map/ppermute | solution.py:220
  341.1 35.8 %collective-permute-start.23 = (bf16[512,512]{1,0:T(8,128)(2,1)S(1)}, bf16[512,512]{1,0:T(8,128)(2,1)S(1)}, u32[]{:S(2)}, u32[]{:S(2)}) collective-permute-start(bf16[512,512]{1,0:T(8,128)(2,1)S(1)} %get-tuple-element.6), channel_id=1, source_target_pairs={{0,8},{4,12},{8,0},{12,4},{1,9},{5,13},{9,1},{13,5},{2,10},{6,14},... | collective-permute-start | bytes 1572872 | tf_op jit(solution)/shard_map/ppermute | solution.py:220
  342.7 42.4 %collective-permute-start.24 = (bf16[512,512]{1,0:T(8,128)(2,1)S(1)}, bf16[512,512]{1,0:T(8,128)(2,1)S(1)}, u32[]{:S(2)}, u32[]{:S(2)}) collective-permute-start(bf16[512,512]{1,0:T(8,128)(2,1)S(1)} %get-tuple-element.5), channel_id=1, source_target_pairs={{0,12},{4,8},{8,4},{12,0},{1,13},{5,9},{9,5},{13,1},{2,14},{6,10},... | collective-permute-start | bytes 1572872 | tf_op jit(solution)/shard_map/ppermute | solution.py:220
  376.9 0.8 copy-start.3
  385.1 0.8 copy-start.5
  386.0 3.7 copy-start.2
  389.7 1.0 copy-start.4
  390.7 1.0 copy-start.6
  391.7 10.0 %copy-start.1 = (bf16[2,256,2304]{2,1,0:T(8,128)(2,1)S(1)}, bf16[2,256,2304]{2,1,0:T(8,128)(2,1)}, u32[]{:S(2)}) copy-start(bf16[2,256,2304]{2,1,0:T(8,128)(2,1)} %param.9) | copy-start | bytes 7077892
Sparse Core Ops, SparseCore 0:
  28.8 43.3 all-gather.2
  75.2 93.0 all-gather.4

commit v2 on v0

v2 whole, which is shorter than its diff:
```python
import functools

import jax
import jax.numpy as jnp
from jax import lax
from jax.experimental import pallas as pl
from jax.experimental.pallas import tpu as pltpu
from jax.sharding import PartitionSpec as P

LOG2E = 1.4426950408889634
WINDOW = 4096
NEG_BIG = -1e30
MESH = pl.DeviceIdType.MESH

HB = 512
HD = 256
HW = 2 * HD
SUB = 256

E1, C1, C2 = 0, 2, 3
WZ, WY, WX, WXY, WC = 5, 6, 7, 8, 9
SHIP_KV, SHIP_Q = 13, 16
SP_Y, SP_OWN, SP_FAR = 19, 23, 27
OZ, OY, OX, OXY, OC = 30, 34, 35, 36, 37
HOME = 40
N_TX = 44


def sublayer_kernel(x_ref, w_ref, wo_ref, y_ref, xbuf, wbuf, webuf, q_buf, kv_buf, made, m_ref, l_ref, acc_ref, o_buf, o_recv, wo_buf, send_sem, recv_sem, load_sem):
    z, r, dp = lax.axis_index("tp"), lax.axis_index("sp"), lax.axis_index("dp")
    z_by = (z, z + 1 - 2 * (z % 2), z + 2 - 4 * (z // 2), 3 - z)
    r1, r2 = r + 1 - 2 * (r % 2), r + 2 - 4 * (r // 2)
    inner = ((z + 1) // 2) % 2
    is_inner, is_edge = inner == 1, inner == 0
    d_model = xbuf.shape[2]
    w_rows, o_rows = d_model // 8, HW // 8

    t_c = inner * (3 - z) + (1 - inner) * z_by[2]
    t_d = inner * z_by[2] + (1 - inner) * (3 - z)
    t_of = (z, z_by[1], t_c, t_d)

    def half_id(t, rr):
        return t + 2 * rr + (t // 2) * (12 - 4 * rr)

    def to(**axes):
        return axes

    over_z = tuple(to(tp=z_by[k]) for k in range(4))
    over_core, over_y, over_x = to(sp=r1), to(sp=r2), to(dp=1 - dp)

    def tx(idx, src, dst, device):
        return pltpu.make_async_remote_copy(src_ref=src, dst_ref=dst, send_sem=send_sem.at[idx], recv_sem=recv_sem.at[idx], device_id=device, device_id_type=MESH)

    def send(idx, src, dst, device):
        tx(idx, src, dst, device).start()

    def arrived(idx, dst):
        tx(idx, dst, dst, over_core).wait_recv()

    def sent(idx, src):
        tx(idx, src, src, over_core).wait_send()

    def rows(n, size):
        return pl.ds(pl.multiple_of(n * size, size), size)

    x_half = [pl.ds(0, HB // 2), pl.ds(HB // 2, HB // 2)]
    piece = dp * 4 + r
    p_y, p_x, p_xy = dp * 4 + r2, (1 - dp) * 4 + r, (1 - dp) * 4 + r2
    pieces_here = (piece, p_y, p_x, p_xy)
    pieces_mate = (dp * 4 + r1, dp * 4 + 3 - r, (1 - dp) * 4 + r1, (1 - dp) * 4 + 3 - r)

    def w_at(p):
        return webuf.at[rows(p, w_rows)]

    def wo_at(p):
        return wo_buf.at[pl.ds(1, 3), rows(p, o_rows)]

    loads = [
        pltpu.make_async_copy(x_ref, xbuf.at[0], load_sem.at[0]),
        pltpu.make_async_copy(w_ref, wbuf, load_sem.at[1]),
        pltpu.make_async_copy(wo_ref, wo_buf.at[0], load_sem.at[2]),
    ]
    for c in loads:
        c.start()

    barrier = pltpu.get_barrier_semaphore()
    peers = over_z[1:] + (over_core, over_y, over_x)
    for peer in peers:
        pl.semaphore_signal(barrier, inc=1, device_id=peer, device_id_type=MESH)
    pl.semaphore_wait(barrier, len(peers))

    @pl.when(is_edge)
    def _():
        send(WZ, w_ref.at[rows(piece, w_rows)], w_at(piece), over_z[1])
        for h in range(2):
            send(E1 + h, x_ref.at[x_half[h]], xbuf.at[1, x_half[h]], over_z[1])

    @pl.when(is_inner)
    def _():
        send(C1, x_ref, xbuf.at[2], over_z[3])

    def project(slot, w, col0, dst):
        def step(n, carry):
            col = pl.multiple_of(n * HD, HD)
            res = jnp.dot(xbuf[slot], w[:, pl.ds(col0 + col, HD)], preferred_element_type=jnp.float32)
            dst[:, pl.ds(col, HD)] = res.astype(jnp.bfloat16)
            return carry

        lax.fori_loop(0, 2, step, 0)

    def kv_slot(j, rr):
        return kv_buf.at[half_id(t_of[j], rr)]

    def spread(j):
        send(SP_Y + j, kv_slot(j, r), kv_slot(j, r), over_y)
        send(SP_OWN + j, kv_slot(j, r), kv_slot(j, r), over_core)

    def spread_on(j):
        arrived(SP_Y + j, kv_slot(j, r2))
        send(SP_FAR + j, kv_slot(j, r2), kv_slot(j, r2), over_core)

    def spread_wait(j):
        arrived(SP_OWN + j, kv_slot(j, r1))
        arrived(SP_FAR + j, kv_slot(j, 3 - r))

    def own_heads(j):
        project(j, wbuf, 0, kv_slot(j, r))
        project(j, wbuf, HW, q_buf.at[t_of[j]])

    def edge_heads(i, j):
        project(j, webuf, 0, made.at[i, 0])
        project(j, webuf, HW, made.at[i, 1])

    def ship(i, j):
        t = t_of[j]
        send(SHIP_KV + i, made.at[i, 0], kv_buf.at[half_id(t, r)], over_z[1])
        send(SHIP_Q + i, made.at[i, 1], q_buf.at[t], over_z[1])

    loads[0].wait()
    loads[1].wait()
    own_heads(0)
    spread(0)
    m_ref[...] = jnp.full(m_ref.shape, NEG_BIG, jnp.float32)
    l_ref[...] = jnp.zeros(l_ref.shape, jnp.float32)
    acc_ref[...] = jnp.zeros(acc_ref.shape, jnp.float32)

    @pl.when(is_inner)
    def _():
        arrived(WZ, w_at(piece))
        send(WX, w_at(piece), w_at(piece), over_x)
        send(WY, w_at(piece), w_at(piece), over_y)
        send(WC, w_at(piece), w_at(piece), over_core)
        arrived(WY, w_at(p_y))
        send(WXY, w_at(p_y), w_at(p_y), over_x)
        send(WC + 1, w_at(p_y), w_at(p_y), over_core)
        arrived(WX, w_at(p_x))
        send(WC + 2, w_at(p_x), w_at(p_x), over_core)
        arrived(E1, xbuf.at[1, x_half[0]])
        send(C2, xbuf.at[1, x_half[0]], xbuf.at[3, x_half[0]], over_z[3])
        arrived(WXY, w_at(p_xy))
        send(WC + 3, w_at(p_xy), w_at(p_xy), over_core)
        for i in range(4):
            arrived(WC + i, w_at(pieces_mate[i]))
        edge_heads(0, 0)
        ship(0, 0)
        arrived(C1, xbuf.at[2])
        own_heads(2)
        spread(2)
        arrived(E1 + 1, xbuf.at[1, x_half[1]])
        send(C2 + 1, xbuf.at[1, x_half[1]], xbuf.at[3, x_half[1]], over_z[3])
        edge_heads(1, 2)
        ship(1, 2)
        own_heads(1)
        spread(1)

    @pl.when(is_edge)
    def _():
        arrived(SHIP_KV, kv_slot(1, r))
        spread(1)
        arrived(SHIP_KV + 1, kv_slot(2, r))
        spread(2)
        arrived(SHIP_Q, q_buf.at[t_of[1]])
        arrived(SHIP_Q + 1, q_buf.at[t_of[2]])

    scale = LOG2E * HD ** -0.5

    def tile(t, g, gap, masked):
        k_blk = kv_buf[g, :, 0:HD]
        v_blk = kv_buf[g, :, HD:HW]
        for sub in range(2 * HB // SUB):
            head, off = divmod(sub * SUB, HB)
            rs = pl.ds(sub * SUB, SUB)
            q_sub = q_buf[t, pl.ds(off, SUB), head * HD:(head + 1) * HD]
            s = lax.dot_general(q_sub, k_blk, (((1,), (1,)), ((), ())), preferred_element_type=jnp.float32)
            if masked:
                dist = gap * HB + off + lax.broadcasted_iota(jnp.int32, (SUB, HB), 0) - lax.broadcasted_iota(jnp.int32, (SUB, HB), 1)
                s = jnp.where((dist >= 0) & (dist < WINDOW), s, -jnp.inf)
            m_old = m_ref[t, rs, :]
            m_new = jnp.maximum(m_old, jnp.max(s, axis=1, keepdims=True))
            alpha = jnp.exp2((m_old - m_new) * scale)
            p = jnp.exp2((s - m_new[:, 0:1]) * scale)
            l_new = p[:, 0:128] + p[:, 128:256] + p[:, 256:384] + p[:, 384:512]
            pv = jnp.dot(p.astype(jnp.bfloat16), v_blk, preferred_element_type=jnp.float32)
            m_ref[t, rs, :] = m_new
            l_ref[t, rs, :] = l_ref[t, rs, :] * alpha + l_new
            acc_ref[t, rs, :] = acc_ref[t, rs, :] * jnp.concatenate([alpha, alpha], axis=1) + pv

    def pick(j):
        return (j == 0) * t_of[0] + (j == 1) * t_of[1] + (j == 2) * t_of[2] + (j == 3) * t_of[3]

    def attend(n, combo):
        def step(i, carry):
            jq, jk = combo(i // 4)
            t = pick(jq)
            g = half_id(pick(jk), i % 4)
            gap = half_id(t, r) - g

            @pl.when((gap > 0) & (gap < 8))
            def _():
                tile(t, g, gap, False)

            @pl.when((gap == 0) | (gap == 8))
            def _():
                tile(t, g, gap, True)

            return carry

        lax.fori_loop(0, 4 * n, step, 0)

    def finish(t):
        for sub in range(2 * HB // SUB):
            head, off = divmod(sub * SUB, HB)
            rs = pl.ds(sub * SUB, SUB)
            total = jnp.sum(l_ref[t, rs, :], axis=1, keepdims=True)
            o_buf[t, pl.ds(off, SUB), head * HD:(head + 1) * HD] = (acc_ref[t, rs, :] / total).astype(jnp.bfloat16)

    for j in range(3):
        spread_on(j)
    spread_wait(0)
    spread_wait(1)
    attend(4, lambda i: (i % 2, i // 2))

    for k in range(1, 4):
        send(OZ + k, wo_ref.at[rows(piece, o_rows)], wo_buf.at[k, rows(piece, o_rows)], over_z[k])

    @pl.when(is_inner)
    def _():
        for h in range(2):
            arrived(C2 + h, xbuf.at[3, x_half[h]])
        project(3, webuf, 0, made.at[2, 0])
        project(3, wbuf, 0, kv_slot(3, r))
        send(SHIP_KV + 2, made.at[2, 0], kv_slot(3, r), over_z[1])
        spread(3)
        project(3, webuf, HW, made.at[2, 1])
        project(3, wbuf, HW, q_buf.at[t_of[3]])
        send(SHIP_Q + 2, made.at[2, 1], q_buf.at[t_of[3]], over_z[1])

    @pl.when(is_edge)
    def _():
        arrived(SHIP_KV + 2, kv_slot(3, r))
        spread(3)

    spread_wait(2)
    attend(5, lambda i: (jnp.minimum(i, 2), jnp.where(i < 3, 2, i - 3)))

    for k in range(1, 4):
        arrived(OZ + k, wo_buf.at[k, rows(piece, o_rows)])
    send(OX, wo_at(piece), wo_at(piece), over_x)
    send(OY, wo_at(piece), wo_at(piece), over_y)
    send(OC, wo_at(piece), wo_at(piece), over_core)

    spread_on(3)

    @pl.when(is_edge)
    def _():
        arrived(SHIP_Q + 2, q_buf.at[t_of[3]])

    spread_wait(3)
    attend(5, lambda i: (jnp.where(i < 4, 3, 2), jnp.minimum(i, 3)))
    for k in range(2, 4):
        finish(z_by[k])
    for k in range(2, 4):
        send(HOME + k, o_buf.at[z_by[k]], o_recv.at[k - 1], over_z[k])
    arrived(OY, wo_at(p_y))
    send(OXY, wo_at(p_y), wo_at(p_y), over_x)
    send(OC + 1, wo_at(p_y), wo_at(p_y), over_core)
    arrived(OX, wo_at(p_x))
    send(OC + 2, wo_at(p_x), wo_at(p_x), over_core)
    attend(2, lambda i: (1 - i, 3))
    finish(z_by[1])
    finish(z)
    send(HOME + 1, o_buf.at[z_by[1]], o_recv.at[0], over_z[1])
    arrived(OXY, wo_at(p_xy))
    send(OC + 3, wo_at(p_xy), wo_at(p_xy), over_core)
    for i in range(4):
        arrived(OC + i, wo_at(pieces_mate[i]))
    loads[2].wait()
    for k in range(1, 4):
        arrived(HOME + k, o_recv.at[k - 1])

    def out_step(n, carry):
        cols = rows(n, HD)
        total = jnp.dot(o_buf[z], wo_buf[0, :, cols], preferred_element_type=jnp.float32)
        for k in range(1, 4):
            total = total + jnp.dot(o_recv[k - 1], wo_buf[k, :, cols], preferred_element_type=jnp.float32)
        y_ref[:, cols] = total.astype(jnp.bfloat16)
        return carry

    lax.fori_loop(0, d_model // HD, out_step, 0)

    @pl.when(is_edge)
    def _():
        sent(WZ, w_at(piece))
        for h in range(2):
            sent(E1 + h, xbuf.at[1, x_half[h]])

    @pl.when(is_inner)
    def _():
        sent(C1, xbuf.at[2])
        for h in range(2):
            sent(C2 + h, xbuf.at[3, x_half[h]])
        for idx in (WY, WX, WXY, WC, WC + 1, WC + 2, WC + 3):
            sent(idx, w_at(piece))
        for i in range(3):
            sent(SHIP_KV + i, made.at[i, 0])
            sent(SHIP_Q + i, made.at[i, 1])

    for j in range(4):
        for base in (SP_Y, SP_OWN, SP_FAR):
            sent(base + j, kv_slot(j, r))
    for k in range(1, 4):
        sent(OZ + k, wo_buf.at[k, rows(piece, o_rows)])
        sent(HOME + k, o_recv.at[k - 1])
    for idx in (OY, OX, OXY, OC, OC + 1, OC + 2, OC + 3):
        sent(idx, wo_at(piece))


def solution(mesh):
    def local_attn(x, w_query, w_key, w_value, w_out):
        d_model = x.shape[1]
        w_own = jnp.concatenate([w_key.reshape(d_model, HD), w_value.reshape(d_model, HD), w_query.reshape(d_model, HW)], axis=1)
        bf16, f32 = jnp.bfloat16, jnp.float32
        return pl.pallas_call(
            sublayer_kernel,
            out_shape=jax.ShapeDtypeStruct((HB, d_model), bf16),
            in_specs=[pl.BlockSpec(memory_space=pl.ANY)] * 3,
            out_specs=pl.BlockSpec(memory_space=pltpu.VMEM),
            scratch_shapes=[
                pltpu.VMEM((4, HB, d_model), bf16),
                pltpu.VMEM((d_model, 2 * HW), bf16),
                pltpu.VMEM((d_model, 2 * HW), bf16),
                pltpu.VMEM((4, HB, HW), bf16),
                pltpu.VMEM((16, HB, HW), bf16),
                pltpu.VMEM((3, 2, HB, HW), bf16),
                pltpu.VMEM((4, 2 * HB, 128), f32),
                pltpu.VMEM((4, 2 * HB, 128), f32),
                pltpu.VMEM((4, 2 * HB, HD), f32),
                pltpu.VMEM((4, HB, HW), bf16),
                pltpu.VMEM((3, HB, HW), bf16),
                pltpu.VMEM((4, HW, d_model), bf16),
                pltpu.SemaphoreType.DMA((N_TX,)),
                pltpu.SemaphoreType.DMA((N_TX,)),
                pltpu.SemaphoreType.DMA((3,)),
            ],
            compiler_params=pltpu.CompilerParams(collective_id=0, has_side_effects=True, vmem_limit_bytes=67043328),
            cost_estimate=pl.CostEstimate(flops=40_000_000_000, bytes_accessed=20_000_000, transcendentals=18_000_000),
            name="sublayer",
        )(x, w_own, w_out.reshape(HW, d_model))

    return jax.shard_map(local_attn, mesh=mesh, in_specs=(P(("dp", "sp", "tp"), None), P(None, "tp", None), P(None, "tp", None), P(None, "tp", None), P("tp", None, None)), out_specs=P(("dp", "sp", "tp"), None), check_vma=False)
```

time: 775 us -> 220 us (0.28)
  the two profiles are of different devices: /device:TPU:26 before, /device:TPU:8 now
where the time goes in v2:
time: 220 us; the launch traced here: 219 us
  Pallas kernels  211 us (96%)
  local copies, waits for them, and re-layouts  5.55 us (3%)
  other arithmetic  2.46 us (1%)
    pallas_call x1, Pallas kernels, local_attn(): pl.pallas_call(sublayer_kernel, out_shape=jax.ShapeDtypeStruct((HB, d_mod...  211 us
    unnamed x6, local copies, waits for them, and re-layouts  5.55 us

profile of v2, /device:TPU:8, one launch (start us, length us, event | category | flops | bytes accessed | tf_op | source)
XLA Modules:
  0.0 219.5 jit_solution(5170562946358167410)
XLA Ops:
  0.0 0.0 copy-start
  0.0 0.0 copy-start.1
  0.0 2.2 %copy.6 = bf16[288,8,2,256]{3,1,2,0:T(8,128)(2,1)S(1)} copy(bf16[288,8,2,256]{3,2,1,0:T(2,128)(2,1)} %bitcast.6) | data formatting | bytes 4718592
  2.2 0.0 copy-done
  2.2 0.1 copy-done.1
  2.3 2.5 %pad_maximum_fusion.w_ref = bf16[2304,1024]{1,0:T(8,128)(2,1)} fusion(bf16[2304,512]{1,0:T(8,128)(2,1)S(1)} %bitcast.5, bf16[2304,256]{1,0:T(8,128)(2,1)S(1)} %bitcast.7, bf16[2304,256]{1,0:T(8,128)(2,1)S(1)} %bitcast.8), kind=kLoop, calls=%fused_computation | loop fusion | flops 14155776 | bytes 9437184 | tf_op jit(solution)/shard_map/concatenate | solution.py:341
  4.8 211.5 %sublayer.1 = bf16[512,2304]{1,0:T(8,128)(2,1)} custom-call(bf16[512,2304]{1,0:T(8,128)(2,1)} %x_ref.1, bf16[2304,1024]{1,0:T(8,128)(2,1)} %pad_maximum_fusion.w_ref, bf16[512,2304]{1,0:T(8,128)(2,1)} %bitcast.9), custom_call_target="tpu_custom_call" | custom-call | flops 40000000000 | bytes 20000000 | tf_op jit(solution)/shard_map/sublayer/pallas_call | solution.py:343
  216.3 3.2 %copy.8 = bf16[512,2304]{1,0:T(8,128)(2,1)} copy(bf16[512,2304]{1,0:T(8,128)(2,1)} %sublayer.1) | data formatting | bytes 4718592
Async XLA Ops:
  0.0 2.2 %copy-start = (bf16[2304,1,256]{2,0,1:T(8,128)(2,1)S(1)}, bf16[2304,1,256]{2,0,1:T(8,128)(2,1)}, u32[]{:S(2)}) copy-start(bf16[2304,1,256]{2,0,1:T(8,128)(2,1)} %param.8) | copy-start | bytes 3538948
  0.0 2.3 %copy-start.1 = (bf16[2304,1,256]{2,0,1:T(8,128)(2,1)S(1)}, bf16[2304,1,256]{2,0,1:T(8,128)(2,1)}, u32[]{:S(2)}) copy-start(bf16[2304,1,256]{2,0,1:T(8,128)(2,1)} %param.7) | copy-start | bytes 3538948

commit v3 on v2

v3 whole, which is shorter than its diff:
```python
import functools

import jax
import jax.numpy as jnp
from jax import lax
from jax.experimental import pallas as pl
from jax.experimental.pallas import tpu as pltpu
from jax.sharding import PartitionSpec as P

LOG2E = 1.4426950408889634
WINDOW = 4096
NEG_BIG = -1e30
MESH = pl.DeviceIdType.MESH

HB = 512
HD = 256
HW = 2 * HD
SUB = 256

_COUNT = (2, 1, 2, 1, 1, 1, 1, 4, 2, 2, 2, 2, 3, 3, 3, 2, 2, 2, 1, 7, 2, 2, 7, 4)
_START = [sum(_COUNT[:i]) for i in range(len(_COUNT))]
E1, C1, C2, WZ, WY, WX, WXY, WC, SHIP_KV, SHIP_Q, SHIPD_KV, SHIPD_Q, SP_Y, SP_OWN, SP_FAR, SPD_Y, SPD_OWN, SPD_FAR, OZ, ONE, OCROSS, OEDGE, TWO, HOME = _START
N_TX = sum(_COUNT)


def sublayer_kernel(x_ref, wk_ref, wv_ref, wq_ref, wo_ref, y_ref, y32, xbuf, wbuf, webuf, q_buf, kv_buf, made, m_ref, l_ref, acc_ref, o_buf, o_recv, wo_buf, send_sem, recv_sem, load_sem):
    z, r, dp = lax.axis_index("tp"), lax.axis_index("sp"), lax.axis_index("dp")
    z_by = (z, z + 1 - 2 * (z % 2), z + 2 - 4 * (z // 2), 3 - z)
    r1, r2 = r + 1 - 2 * (r % 2), r + 2 - 4 * (r // 2)
    inner = ((z + 1) // 2) % 2
    is_inner, is_edge = inner == 1, inner == 0
    d_model = xbuf.shape[2]
    w_rows, o_rows = d_model // 8, HW // 8

    t_c = inner * (3 - z) + (1 - inner) * z_by[2]
    t_d = inner * z_by[2] + (1 - inner) * (3 - z)
    t_of = (z, z_by[1], t_c, t_d)

    def half_id(t, rr):
        return t + 2 * rr + (t // 2) * (12 - 4 * rr)

    def to(**axes):
        return axes

    over_z = tuple(to(tp=z_by[k]) for k in range(4))
    over_core, over_y, over_x = to(sp=r1), to(sp=r2), to(dp=1 - dp)

    def tx(idx, src, dst, device):
        return pltpu.make_async_remote_copy(src_ref=src, dst_ref=dst, send_sem=send_sem.at[idx], recv_sem=recv_sem.at[idx], device_id=device, device_id_type=MESH)

    def send(idx, src, dst, device):
        tx(idx, src, dst, device).start()

    def arrived(idx, dst):
        tx(idx, dst, dst, over_core).wait_recv()

    def sent(idx, src):
        tx(idx, src, src, over_core).wait_send()

    def rows(n, size):
        return pl.ds(pl.multiple_of(n * size, size), size)

    x_half = [pl.ds(0, HB // 2), pl.ds(HB // 2, HB // 2)]
    piece = dp * 4 + r
    p_y, p_x, p_xy = dp * 4 + r2, (1 - dp) * 4 + r, (1 - dp) * 4 + r2
    pieces_here = (piece, p_y, p_x, p_xy)
    pieces_mate = (dp * 4 + r1, dp * 4 + 3 - r, (1 - dp) * 4 + r1, (1 - dp) * 4 + 3 - r)

    def w_at(p):
        return webuf.at[rows(p, w_rows)]

    def wo_at(first, n, p):
        return wo_buf.at[pl.ds(first, n), rows(p, o_rows)]

    loads = [
        pltpu.make_async_copy(wk_ref, wbuf.at[:, 0:HD], load_sem.at[0]),
        pltpu.make_async_copy(wv_ref, wbuf.at[:, HD:HW], load_sem.at[1]),
        pltpu.make_async_copy(wq_ref, wbuf.at[:, HW:2 * HW], load_sem.at[2]),
        pltpu.make_async_copy(x_ref, xbuf.at[0], load_sem.at[3]),
        pltpu.make_async_copy(wo_ref, wo_buf.at[0], load_sem.at[4]),
    ]
    for c in loads:
        c.start()

    barrier = pltpu.get_barrier_semaphore()
    peers = over_z[1:] + (over_core, over_y, over_x)
    for peer in peers:
        pl.semaphore_signal(barrier, inc=1, device_id=peer, device_id_type=MESH)
    pl.semaphore_wait(barrier, len(peers))

    @pl.when(is_inner)
    def _():
        send(C1, x_ref, xbuf.at[2], over_z[3])

    for c in loads[:3]:
        c.wait()

    def out_edge():
        send(OZ, wo_ref.at[rows(piece, o_rows)], wo_buf.at[1, rows(piece, o_rows)], over_z[1])

    @pl.when(is_edge)
    def _():
        send(WZ, wbuf.at[rows(piece, w_rows)], w_at(piece), over_z[1])
        send(E1, x_ref.at[x_half[0]], xbuf.at[1, x_half[0]], over_z[1])
        out_edge()
        send(E1 + 1, x_ref.at[x_half[1]], xbuf.at[1, x_half[1]], over_z[1])

    @pl.when(is_inner)
    def _():
        out_edge()

    def project(slot, part, w, col0, dst):
        def step(n, carry):
            col = pl.multiple_of(n * HD, HD)
            res = jnp.dot(xbuf[slot, part, :], w[:, pl.ds(col0 + col, HD)], preferred_element_type=jnp.float32)
            dst[:, pl.ds(col, HD)] = res.astype(jnp.bfloat16)
            return carry

        lax.fori_loop(0, 2, step, 0)

    whole = pl.ds(0, HB)

    def kv_slot(j, rr):
        return kv_buf.at[half_id(t_of[j], rr)]

    def kvd(h, rr):
        return kv_buf.at[half_id(t_of[3], rr), x_half[h]]

    def spread(j):
        send(SP_Y + j, kv_slot(j, r), kv_slot(j, r), over_y)
        send(SP_OWN + j, kv_slot(j, r), kv_slot(j, r), over_core)

    def spread_on(j):
        arrived(SP_Y + j, kv_slot(j, r2))
        send(SP_FAR + j, kv_slot(j, r2), kv_slot(j, r2), over_core)

    def spread_wait(j):
        arrived(SP_OWN + j, kv_slot(j, r1))
        arrived(SP_FAR + j, kv_slot(j, 3 - r))

    def spread_last(h):
        send(SPD_Y + h, kvd(h, r), kvd(h, r), over_y)
        send(SPD_OWN + h, kvd(h, r), kvd(h, r), over_core)

    def spread_last_on(h):
        arrived(SPD_Y + h, kvd(h, r2))
        send(SPD_FAR + h, kvd(h, r2), kvd(h, r2), over_core)

    def spread_last_wait(h):
        arrived(SPD_OWN + h, kvd(h, r1))
        arrived(SPD_FAR + h, kvd(h, 3 - r))

    def own_heads(j):
        project(j, whole, wbuf, 0, kv_slot(j, r))
        project(j, whole, wbuf, HW, q_buf.at[t_of[j]])

    def edge_heads(i, j):
        t = t_of[j]
        project(j, whole, webuf, 0, made.at[i, 0])
        project(j, whole, webuf, HW, made.at[i, 1])
        send(SHIP_KV + i, made.at[i, 0], kv_buf.at[half_id(t, r)], over_z[1])
        send(SHIP_Q + i, made.at[i, 1], q_buf.at[t], over_z[1])

    def last_rows(h):
        part = x_half[h]
        arrived(C2 + h, xbuf.at[3, part])
        project(3, part, webuf, 0, made.at[2, 0, part])
        project(3, part, wbuf, 0, kvd(h, r))
        send(SHIPD_KV + h, made.at[2, 0, part], kvd(h, r), over_z[1])
        spread_last(h)
        project(3, part, webuf, HW, made.at[2, 1, part])
        project(3, part, wbuf, HW, q_buf.at[t_of[3], part])
        send(SHIPD_Q + h, made.at[2, 1, part], q_buf.at[t_of[3], part], over_z[1])

    def out_hop(base, first, n):
        send(base, wo_at(first, n, piece), wo_at(first, n, piece), over_x)
        send(base + 1, wo_at(first, n, piece), wo_at(first, n, piece), over_y)
        send(base + 3, wo_at(first, n, piece), wo_at(first, n, piece), over_core)

    def out_hop2(base, first, n):
        arrived(base + 1, wo_at(first, n, p_y))
        send(base + 2, wo_at(first, n, p_y), wo_at(first, n, p_y), over_x)
        send(base + 4, wo_at(first, n, p_y), wo_at(first, n, p_y), over_core)
        arrived(base, wo_at(first, n, p_x))
        send(base + 5, wo_at(first, n, p_x), wo_at(first, n, p_x), over_core)

    def out_hop3(base, first, n):
        arrived(base + 2, wo_at(first, n, p_xy))
        send(base + 6, wo_at(first, n, p_xy), wo_at(first, n, p_xy), over_core)

    def out_wait(base, first, n):
        for i in range(4):
            arrived(base + 3 + i, wo_at(first, n, pieces_mate[i]))

    loads[3].wait()
    own_heads(0)
    spread(0)
    m_ref[...] = jnp.full(m_ref.shape, NEG_BIG, jnp.float32)
    l_ref[...] = jnp.zeros(l_ref.shape, jnp.float32)
    acc_ref[...] = jnp.zeros(acc_ref.shape, jnp.float32)

    @pl.when(is_inner)
    def _():
        arrived(WZ, w_at(piece))
        send(WX, w_at(piece), w_at(piece), over_x)
        send(WY, w_at(piece), w_at(piece), over_y)
        send(WC, w_at(piece), w_at(piece), over_core)
        arrived(WY, w_at(p_y))
        send(WXY, w_at(p_y), w_at(p_y), over_x)
        send(WC + 1, w_at(p_y), w_at(p_y), over_core)
        arrived(WX, w_at(p_x))
        send(WC + 2, w_at(p_x), w_at(p_x), over_core)
        spread_on(0)
        arrived(E1, xbuf.at[1, x_half[0]])
        send(C2, xbuf.at[1, x_half[0]], xbuf.at[3, x_half[0]], over_z[3])
        arrived(WXY, w_at(p_xy))
        send(WC + 3, w_at(p_xy), w_at(p_xy), over_core)
        for i in range(4):
            arrived(WC + i, w_at(pieces_mate[i]))
        edge_heads(0, 0)
        arrived(OZ, wo_buf.at[1, rows(piece, o_rows)])
        out_hop(ONE, 1, 1)
        arrived(C1, xbuf.at[2])
        own_heads(2)
        spread(2)
        arrived(E1 + 1, xbuf.at[1, x_half[1]])
        send(C2 + 1, xbuf.at[1, x_half[1]], xbuf.at[3, x_half[1]], over_z[3])
        send(OCROSS, wo_ref.at[rows(piece, o_rows)], wo_buf.at[3, rows(piece, o_rows)], over_z[3])
        send(OCROSS + 1, wo_buf.at[1, rows(piece, o_rows)], wo_buf.at[2, rows(piece, o_rows)], over_z[3])
        edge_heads(1, 2)
        own_heads(1)
        spread(1)
        spread_on(2)
        last_rows(0)
        spread_on(1)

    @pl.when(is_edge)
    def _():
        arrived(OZ, wo_buf.at[1, rows(piece, o_rows)])
        out_hop(ONE, 1, 1)
        spread_on(0)
        arrived(SHIP_KV, kv_slot(1, r))
        spread(1)
        arrived(SHIP_Q, q_buf.at[t_of[1]])
        spread_on(1)
        arrived(SHIP_KV + 1, kv_slot(2, r))
        spread(2)

    scale = LOG2E * HD ** -0.5

    def tile(t, g, gap, masked):
        k_blk = kv_buf[g, :, 0:HD]
        v_blk = kv_buf[g, :, HD:HW]
        n_sub = 2 * HB // SUB

        def scores(sub):
            head, off = divmod(sub * SUB, HB)
            q_sub = q_buf[t, pl.ds(off, SUB), head * HD:(head + 1) * HD]
            return lax.dot_general(q_sub, k_blk, (((1,), (1,)), ((), ())), preferred_element_type=jnp.float32)

        ahead = scores(0)
        for sub in range(n_sub):
            off = sub * SUB % HB
            rs = pl.ds(sub * SUB, SUB)
            s = ahead
            if sub + 1 < n_sub:
                ahead = scores(sub + 1)
            if masked:
                dist = gap * HB + off + lax.broadcasted_iota(jnp.int32, (SUB, HB), 0) - lax.broadcasted_iota(jnp.int32, (SUB, HB), 1)
                s = jnp.where((dist >= 0) & (dist < WINDOW), s, -jnp.inf)
            m_old = m_ref[t, rs, :]
            m_new = jnp.maximum(m_old, jnp.max(s, axis=1, keepdims=True))
            alpha = jnp.exp2((m_old - m_new) * scale)
            p = jnp.exp2((s - jnp.concatenate([m_new] * 4, axis=1)) * scale)
            l_new = p[:, 0:128] + p[:, 128:256] + p[:, 256:384] + p[:, 384:512]
            pv = jnp.dot(p.astype(jnp.bfloat16), v_blk, preferred_element_type=jnp.float32)
            m_ref[t, rs, :] = m_new
            l_ref[t, rs, :] = l_ref[t, rs, :] * alpha + l_new
            acc_ref[t, rs, :] = acc_ref[t, rs, :] * jnp.concatenate([alpha, alpha], axis=1) + pv

    def pick(j):
        return (j == 0) * t_of[0] + (j == 1) * t_of[1] + (j == 2) * t_of[2] + (j == 3) * t_of[3]

    def attend(n, combo):
        def step(i, carry):
            jq, jk = combo(i // 4)
            t = pick(jq)
            g = half_id(pick(jk), i % 4)
            gap = half_id(t, r) - g

            @pl.when((gap > 0) & (gap < 8))
            def _():
                tile(t, g, gap, False)

            @pl.when((gap == 0) | (gap == 8))
            def _():
                tile(t, g, gap, True)

            return carry

        lax.fori_loop(0, 4 * n, step, 0)

    def finish(t):
        for sub in range(2 * HB // SUB):
            head, off = divmod(sub * SUB, HB)
            rs = pl.ds(sub * SUB, SUB)
            total = jnp.sum(l_ref[t, rs, :], axis=1, keepdims=True)
            o_buf[t, pl.ds(off, SUB), head * HD:(head + 1) * HD] = (acc_ref[t, rs, :] / total).astype(jnp.bfloat16)

    spread_wait(0)
    spread_wait(1)
    attend(4 * (1 - inner), lambda i: (i % 2, i // 2))

    @pl.when(is_edge)
    def _():
        arrived(SHIPD_KV, kvd(0, r))
        spread_last(0)
        spread_on(2)
        arrived(SHIP_Q + 1, q_buf.at[t_of[2]])

    out_hop2(ONE, 1, 1)
    spread_wait(2)
    attend(3, lambda i: (2, i))
    spread_last_on(0)

    @pl.when(is_inner)
    def _():
        last_rows(1)

    @pl.when(is_edge)
    def _():
        arrived(SHIPD_KV + 1, kvd(1, r))
        spread_last(1)
        for h in range(2):
            arrived(SHIPD_Q + h, q_buf.at[t_of[3], x_half[h]])

    out_hop3(ONE, 1, 1)
    attend(3, lambda i: (3, i))
    spread_last_on(1)
    for h in range(2):
        spread_last_wait(h)
    attend(1, lambda i: (2, 3))
    finish(t_c)

    def home(t, by_inner, by_edge):
        @pl.when(is_inner)
        def _():
            send(HOME + by_inner, o_buf.at[t], o_recv.at[by_inner - 1], over_z[by_inner])

        @pl.when(is_edge)
        def _():
            send(HOME + by_edge, o_buf.at[t], o_recv.at[by_edge - 1], over_z[by_edge])

    home(t_c, 3, 2)

    @pl.when(is_inner)
    def _():
        for i in range(2):
            arrived(OCROSS + i, wo_buf.at[3 - i, rows(piece, o_rows)])
            send(OEDGE + i, wo_buf.at[3 - i, rows(piece, o_rows)], wo_buf.at[2 + i, rows(piece, o_rows)], over_z[1])

    attend(1, lambda i: (3, 3))
    finish(t_d)
    home(t_d, 2, 3)

    @pl.when(is_edge)
    def _():
        for i in range(2):
            arrived(OEDGE + i, wo_buf.at[2 + i, rows(piece, o_rows)])

    out_hop(TWO, 2, 2)
    attend(4 + 4 * inner, lambda i: (i % 2, (i // 2 + 2) % 4))
    finish(z_by[1])
    finish(z)
    send(HOME + 1, o_buf.at[z_by[1]], o_recv.at[0], over_z[1])
    out_hop2(TWO, 2, 2)
    out_wait(ONE, 1, 1)
    loads[4].wait()
    arrived(HOME + 1, o_recv.at[0])

    def out_near(n, carry):
        cols = rows(n, HD)
        near = jnp.dot(o_buf[z], wo_buf[0, :, cols], preferred_element_type=jnp.float32)
        y32[:, cols] = near + jnp.dot(o_recv[0], wo_buf[1, :, cols], preferred_element_type=jnp.float32)
        return carry

    lax.fori_loop(0, d_model // HD, out_near, 0)
    out_hop3(TWO, 2, 2)
    out_wait(TWO, 2, 2)
    for k in range(2, 4):
        arrived(HOME + k, o_recv.at[k - 1])

    def out_far(n, carry):
        cols = rows(n, HD)
        far = jnp.dot(o_recv[1], wo_buf[2, :, cols], preferred_element_type=jnp.float32)
        far = far + jnp.dot(o_recv[2], wo_buf[3, :, cols], preferred_element_type=jnp.float32)
        y_ref[:, cols] = (y32[:, cols] + far).astype(jnp.bfloat16)
        return carry

    lax.fori_loop(0, d_model // HD, out_far, 0)

    @pl.when(is_edge)
    def _():
        sent(WZ, w_at(piece))
        for h in range(2):
            sent(E1 + h, xbuf.at[1, x_half[h]])

    @pl.when(is_inner)
    def _():
        sent(C1, xbuf.at[2])
        for h in range(2):
            sent(C2 + h, xbuf.at[3, x_half[h]])
            sent(SHIPD_KV + h, made.at[2, 0, x_half[h]])
            sent(SHIPD_Q + h, made.at[2, 1, x_half[h]])
            sent(SHIP_KV + h, made.at[h, 0])
            sent(SHIP_Q + h, made.at[h, 1])
            sent(OCROSS + h, wo_buf.at[2 + h, rows(piece, o_rows)])
            sent(OEDGE + h, wo_buf.at[2 + h, rows(piece, o_rows)])
        for idx in (WY, WX, WXY, WC, WC + 1, WC + 2, WC + 3):
            sent(idx, w_at(piece))

    for j in range(3):
        for base in (SP_Y, SP_OWN, SP_FAR):
            sent(base + j, kv_slot(j, r))
    for h in range(2):
        for base in (SPD_Y, SPD_OWN, SPD_FAR):
            sent(base + h, kvd(h, r))
    sent(OZ, wo_buf.at[1, rows(piece, o_rows)])
    for i in range(7):
        sent(ONE + i, wo_at(1, 1, piece))
        sent(TWO + i, wo_at(2, 2, piece))
    for k in range(1, 4):
        sent(HOME + k, o_recv.at[k - 1])


def solution(mesh):
    def local_attn(x, w_query, w_key, w_value, w_out):
        d_model = x.shape[1]
        bf16, f32 = jnp.bfloat16, jnp.float32
        return pl.pallas_call(
            sublayer_kernel,
            out_shape=jax.ShapeDtypeStruct((HB, d_model), bf16),
            in_specs=[pl.BlockSpec(memory_space=pl.ANY)] * 5,
            out_specs=pl.BlockSpec(memory_space=pltpu.VMEM),
            scratch_shapes=[
                pltpu.VMEM((HB, d_model), f32),
                pltpu.VMEM((4, HB, d_model), bf16),
                pltpu.VMEM((d_model, 2 * HW), bf16),
                pltpu.VMEM((d_model, 2 * HW), bf16),
                pltpu.VMEM((4, HB, HW), bf16),
                pltpu.VMEM((16, HB, HW), bf16),
                pltpu.VMEM((3, 2, HB, HW), bf16),
                pltpu.VMEM((4, 2 * HB, 128), f32),
                pltpu.VMEM((4, 2 * HB, 128), f32),
                pltpu.VMEM((4, 2 * HB, HD), f32),
                pltpu.VMEM((4, HB, HW), bf16),
                pltpu.VMEM((3, HB, HW), bf16),
                pltpu.VMEM((4, HW, d_model), bf16),
                pltpu.SemaphoreType.DMA((N_TX,)),
                pltpu.SemaphoreType.DMA((N_TX,)),
                pltpu.SemaphoreType.DMA((5,)),
            ],
            compiler_params=pltpu.CompilerParams(collective_id=0, has_side_effects=True, vmem_limit_bytes=67043328),
            cost_estimate=pl.CostEstimate(flops=40_000_000_000, bytes_accessed=20_000_000, transcendentals=18_000_000),
            name="sublayer",
        )(x, w_key.reshape(d_model, HD), w_value.reshape(d_model, HD), w_query.reshape(d_model, HW), w_out.reshape(HW, d_model))

    return jax.shard_map(local_attn, mesh=mesh, in_specs=(P(("dp", "sp", "tp"), None), P(None, "tp", None), P(None, "tp", None), P(None, "tp", None), P("tp", None, None)), out_specs=P(("dp", "sp", "tp"), None), check_vma=False)
```

time: 220 us -> 193 us (0.88)
  the two profiles are of different devices: /device:TPU:8 before, /device:TPU:26 now
where the time goes in v3:
time: 193 us; the launch traced here: 191 us
  Pallas kernels  184 us (95%)
  local copies, waits for them, and re-layouts  6.68 us (3%)
    pallas_call x1, Pallas kernels, local_attn(): pl.pallas_call(sublayer_kernel, out_shape=jax.ShapeDtypeStruct((HB, d_mod...  184 us
    unnamed x2, local copies, waits for them, and re-layouts  6.68 us

profile of v3, /device:TPU:26, one launch (start us, length us, event | category | flops | bytes accessed | tf_op | source)
XLA Modules:
  0.0 190.6 jit_solution(9670046325599144497)
XLA Ops:
  0.0 3.5 %copy.6 = bf16[288,8,2,256]{3,1,2,0:T(8,128)(2,1)} copy(bf16[288,8,2,256]{3,2,1,0:T(2,128)(2,1)} %bitcast.5) | data formatting | bytes 4718592
  3.5 183.9 %sublayer.1 = bf16[512,2304]{1,0:T(8,128)(2,1)} custom-call(bf16[512,2304]{1,0:T(8,128)(2,1)} %x_ref.1, bf16[2304,256]{1,0:T(8,128)(2,1)} %bitcast.8, bf16[2304,256]{1,0:T(8,128)(2,1)} %bitcast.9, bf16[2304,512]{1,0:T(8,128)(2,1)} %bitcast.6, bf16[512,2304]{1,0:T(8,128)(2,1)} %bitcast.7), custom_call_target="tpu_custom_call" | custom-call | flops 40000000000 | bytes 20000000 | tf_op jit(solution)/shard_map/sublayer/pallas_call | solution.py:440
  187.3 3.2 %copy.8 = bf16[512,2304]{1,0:T(8,128)(2,1)} copy(bf16[512,2304]{1,0:T(8,128)(2,1)} %sublayer.1) | data formatting | bytes 4718592

commit v4 on v3

--- a/solution.py
+++ b/solution.py
@@ -17,7 +17,7 @@
 HW = 2 * HD
 SUB = 256
 
-_COUNT = (2, 1, 2, 1, 1, 1, 1, 4, 2, 2, 2, 2, 3, 3, 3, 2, 2, 2, 1, 7, 2, 2, 7, 4)
+_COUNT = (2, 1, 3, 1, 1, 1, 1, 4, 2, 2, 3, 3, 3, 3, 3, 3, 3, 3, 1, 7, 2, 2, 7, 4)
 _START = [sum(_COUNT[:i]) for i in range(len(_COUNT))]
 E1, C1, C2, WZ, WY, WX, WXY, WC, SHIP_KV, SHIP_Q, SHIPD_KV, SHIPD_Q, SP_Y, SP_OWN, SP_FAR, SPD_Y, SPD_OWN, SPD_FAR, OZ, ONE, OCROSS, OEDGE, TWO, HOME = _START
 N_TX = sum(_COUNT)
@@ -61,6 +61,7 @@
         return pl.ds(pl.multiple_of(n * size, size), size)
 
     x_half = [pl.ds(0, HB // 2), pl.ds(HB // 2, HB // 2)]
+    x_part = [pl.ds(0, HB // 2), pl.ds(HB // 2, HB // 4), pl.ds(3 * HB // 4, HB // 4)]
     piece = dp * 4 + r
     p_y, p_x, p_xy = dp * 4 + r2, (1 - dp) * 4 + r, (1 - dp) * 4 + r2
     pieces_here = (piece, p_y, p_x, p_xy)
@@ -124,7 +125,7 @@
         return kv_buf.at[half_id(t_of[j], rr)]
 
     def kvd(h, rr):
-        return kv_buf.at[half_id(t_of[3], rr), x_half[h]]
+        return kv_buf.at[half_id(t_of[3], rr), x_part[h]]
 
     def spread(j):
         send(SP_Y + j, kv_slot(j, r), kv_slot(j, r), over_y)
@@ -162,7 +163,7 @@
         send(SHIP_Q + i, made.at[i, 1], q_buf.at[t], over_z[1])
 
     def last_rows(h):
-        part = x_half[h]
+        part = x_part[h]
         arrived(C2 + h, xbuf.at[3, part])
         project(3, part, webuf, 0, made.at[2, 0, part])
         project(3, part, wbuf, 0, kvd(h, r))
@@ -224,7 +225,8 @@
         own_heads(2)
         spread(2)
         arrived(E1 + 1, xbuf.at[1, x_half[1]])
-        send(C2 + 1, xbuf.at[1, x_half[1]], xbuf.at[3, x_half[1]], over_z[3])
+        for h in range(1, 3):
+            send(C2 + h, xbuf.at[1, x_part[h]], xbuf.at[3, x_part[h]], over_z[3])
         send(OCROSS, wo_ref.at[rows(piece, o_rows)], wo_buf.at[3, rows(piece, o_rows)], over_z[3])
         send(OCROSS + 1, wo_buf.at[1, rows(piece, o_rows)], wo_buf.at[2, rows(piece, o_rows)], over_z[3])
         edge_heads(1, 2)
@@ -326,18 +328,19 @@
     @pl.when(is_inner)
     def _():
         last_rows(1)
-
-    @pl.when(is_edge)
-    def _():
-        arrived(SHIPD_KV + 1, kvd(1, r))
-        spread_last(1)
-        for h in range(2):
-            arrived(SHIPD_Q + h, q_buf.at[t_of[3], x_half[h]])
+        last_rows(2)
+
+    @pl.when(is_edge)
+    def _():
+        for h in range(1, 3):
+            arrived(SHIPD_KV + h, kvd(h, r))
+            spread_last(h)
 
     out_hop3(ONE, 1, 1)
-    attend(3, lambda i: (3, i))
     spread_last_on(1)
-    for h in range(2):
+    attend(3 * inner, lambda i: (3, i))
+    spread_last_on(2)
+    for h in range(3):
         spread_last_wait(h)
     attend(1, lambda i: (2, 3))
     finish(t_c)
@@ -359,7 +362,12 @@
             arrived(OCROSS + i, wo_buf.at[3 - i, rows(piece, o_rows)])
             send(OEDGE + i, wo_buf.at[3 - i, rows(piece, o_rows)], wo_buf.at[2 + i, rows(piece, o_rows)], over_z[1])
 
-    attend(1, lambda i: (3, 3))
+    @pl.when(is_edge)
+    def _():
+        for h in range(3):
+            arrived(SHIPD_Q + h, q_buf.at[t_of[3], x_part[h]])
+
+    attend(4 - 3 * inner, lambda i: (3, (i + 3) % 4))
     finish(t_d)
     home(t_d, 2, 3)
 
@@ -408,10 +416,11 @@
     @pl.when(is_inner)
     def _():
         sent(C1, xbuf.at[2])
+        for h in range(3):
+            sent(C2 + h, xbuf.at[3, x_part[h]])
+            sent(SHIPD_KV + h, made.at[2, 0, x_part[h]])
+            sent(SHIPD_Q + h, made.at[2, 1, x_part[h]])
         for h in range(2):
-            sent(C2 + h, xbuf.at[3, x_half[h]])
-            sent(SHIPD_KV + h, made.at[2, 0, x_half[h]])
-            sent(SHIPD_Q + h, made.at[2, 1, x_half[h]])
             sent(SHIP_KV + h, made.at[h, 0])
             sent(SHIP_Q + h, made.at[h, 1])
             sent(OCROSS + h, wo_buf.at[2 + h, rows(piece, o_rows)])
@@ -422,7 +431,7 @@
     for j in range(3):
         for base in (SP_Y, SP_OWN, SP_FAR):
             sent(base + j, kv_slot(j, r))
-    for h in range(2):
+    for h in range(3):
         for base in (SPD_Y, SPD_OWN, SPD_FAR):
             sent(base + h, kvd(h, r))
     sent(OZ, wo_buf.at[1, rows(piece, o_rows)])

time: 193 us -> 194 us (level)
  Pallas kernels: 184 us -> 186 us
    pallas_call x1, Pallas kernels: 184 us -> 186 us  [local_attn(): pl.pallas_call(sublayer_kernel, out_shape=jax.ShapeDtypeStruct((HB, d_mod...]
where the time goes in v4:
time: 194 us; the launch traced here: 193 us
  Pallas kernels  186 us (96%)
  local copies, waits for them, and re-layouts  6.68 us (3%)
    pallas_call x1, Pallas kernels, local_attn(): pl.pallas_call(sublayer_kernel, out_shape=jax.ShapeDtypeStruct((HB, d_mod...  186 us
    unnamed x2, local copies, waits for them, and re-layouts  6.68 us

profile of v4, /device:TPU:26, one launch (start us, length us, event | category | flops | bytes accessed | tf_op | source)
XLA Modules:
  0.0 192.5 jit_solution(6586072060392288738)
XLA Ops:
  0.0 3.5 %copy.6 = bf16[288,8,2,256]{3,1,2,0:T(8,128)(2,1)} copy(bf16[288,8,2,256]{3,2,1,0:T(2,128)(2,1)} %bitcast.5) | data formatting | bytes 4718592
  3.5 185.8 %sublayer.1 = bf16[512,2304]{1,0:T(8,128)(2,1)} custom-call(bf16[512,2304]{1,0:T(8,128)(2,1)} %x_ref.1, bf16[2304,256]{1,0:T(8,128)(2,1)} %bitcast.8, bf16[2304,256]{1,0:T(8,128)(2,1)} %bitcast.9, bf16[2304,512]{1,0:T(8,128)(2,1)} %bitcast.6, bf16[512,2304]{1,0:T(8,128)(2,1)} %bitcast.7), custom_call_target="tpu_custom_call" | custom-call | flops 40000000000 | bytes 20000000 | tf_op jit(solution)/shard_map/sublayer/pallas_call | solution.py:449
  189.3 3.2 %copy.8 = bf16[512,2304]{1,0:T(8,128)(2,1)} copy(bf16[512,2304]{1,0:T(8,128)(2,1)} %sublayer.1) | data formatting | bytes 4718592

commit v5 on v4

--- a/solution.py
+++ b/solution.py
@@ -17,7 +17,7 @@
 HW = 2 * HD
 SUB = 256
 
-_COUNT = (2, 1, 3, 1, 1, 1, 1, 4, 2, 2, 3, 3, 3, 3, 3, 3, 3, 3, 1, 7, 2, 2, 7, 4)
+_COUNT = (2, 1, 3, 1, 1, 1, 1, 4, 2, 2, 3, 3, 3, 3, 3, 3, 3, 3, 1, 7, 2, 2, 8, 4)
 _START = [sum(_COUNT[:i]) for i in range(len(_COUNT))]
 E1, C1, C2, WZ, WY, WX, WXY, WC, SHIP_KV, SHIP_Q, SHIPD_KV, SHIPD_Q, SP_Y, SP_OWN, SP_FAR, SPD_Y, SPD_OWN, SPD_FAR, OZ, ONE, OCROSS, OEDGE, TWO, HOME = _START
 N_TX = sum(_COUNT)
@@ -188,6 +188,19 @@
     def out_hop3(base, first, n):
         arrived(base + 2, wo_at(first, n, p_xy))
         send(base + 6, wo_at(first, n, p_xy), wo_at(first, n, p_xy), over_core)
+
+    def out_hop2_far():
+        arrived(TWO + 1, wo_at(2, 2, p_y))
+        send(TWO + 2, wo_at(2, 1, p_y), wo_at(2, 1, p_y), over_x)
+        send(TWO + 4, wo_at(2, 2, p_y), wo_at(2, 2, p_y), over_core)
+        arrived(TWO, wo_at(2, 2, p_x))
+        send(TWO + 7, wo_at(3, 1, p_x), wo_at(3, 1, p_x), over_y)
+        send(TWO + 5, wo_at(2, 2, p_x), wo_at(2, 2, p_x), over_core)
+
+    def out_hop3_far():
+        arrived(TWO + 2, wo_at(2, 1, p_xy))
+        arrived(TWO + 7, wo_at(3, 1, p_xy))
+        send(TWO + 6, wo_at(2, 2, p_xy), wo_at(2, 2, p_xy), over_core)
 
     def out_wait(base, first, n):
         for i in range(4):
@@ -381,19 +394,25 @@
     finish(z_by[1])
     finish(z)
     send(HOME + 1, o_buf.at[z_by[1]], o_recv.at[0], over_z[1])
-    out_hop2(TWO, 2, 2)
+    out_hop2_far()
+    loads[4].wait()
+
+    def out_own(n, carry):
+        cols = rows(n, HD)
+        y32[:, cols] = jnp.dot(o_buf[z], wo_buf[0, :, cols], preferred_element_type=jnp.float32)
+        return carry
+
+    lax.fori_loop(0, d_model // HD, out_own, 0)
+    out_hop3_far()
     out_wait(ONE, 1, 1)
-    loads[4].wait()
     arrived(HOME + 1, o_recv.at[0])
 
     def out_near(n, carry):
         cols = rows(n, HD)
-        near = jnp.dot(o_buf[z], wo_buf[0, :, cols], preferred_element_type=jnp.float32)
-        y32[:, cols] = near + jnp.dot(o_recv[0], wo_buf[1, :, cols], preferred_element_type=jnp.float32)
+        y32[:, cols] = y32[:, cols] + jnp.dot(o_recv[0], wo_buf[1, :, cols], preferred_element_type=jnp.float32)
         return carry
 
     lax.fori_loop(0, d_model // HD, out_near, 0)
-    out_hop3(TWO, 2, 2)
     out_wait(TWO, 2, 2)
     for k in range(2, 4):
         arrived(HOME + k, o_recv.at[k - 1])
@@ -437,7 +456,8 @@
     sent(OZ, wo_buf.at[1, rows(piece, o_rows)])
     for i in range(7):
         sent(ONE + i, wo_at(1, 1, piece))
-        sent(TWO + i, wo_at(2, 2, piece))
+    for i in range(8):
+        sent(TWO + i, wo_at(2, 1 if i in (2, 7) else 2, piece))
     for k in range(1, 4):
         sent(HOME + k, o_recv.at[k - 1])
 

time: 194 us -> 190 us (0.979)
  Pallas kernels: 186 us -> 184 us
    pallas_call x1, Pallas kernels: 186 us -> 184 us  [local_attn(): pl.pallas_call(sublayer_kernel, out_shape=jax.ShapeDtypeStruct((HB, d_mod...]
where the time goes in v5:
time: 190 us
  Pallas kernels  184 us (97%)
  local copies, waits for them, and re-layouts  6.68 us (4%)
    pallas_call x1, Pallas kernels, local_attn(): pl.pallas_call(sublayer_kernel, out_shape=jax.ShapeDtypeStruct((HB, d_mod...  184 us
    unnamed x2, local copies, waits for them, and re-layouts  6.68 us

profile of v5, /device:TPU:26, one launch (start us, length us, event | category | flops | bytes accessed | tf_op | source)
XLA Modules:
  0.0 190.3 jit_solution(6829347106814561886)
XLA Ops:
  0.0 3.5 %copy.6 = bf16[288,8,2,256]{3,1,2,0:T(8,128)(2,1)} copy(bf16[288,8,2,256]{3,2,1,0:T(2,128)(2,1)} %bitcast.5) | data formatting | bytes 4718592
  3.5 183.6 %sublayer.1 = bf16[512,2304]{1,0:T(8,128)(2,1)} custom-call(bf16[512,2304]{1,0:T(8,128)(2,1)} %x_ref.1, bf16[2304,256]{1,0:T(8,128)(2,1)} %bitcast.8, bf16[2304,256]{1,0:T(8,128)(2,1)} %bitcast.9, bf16[2304,512]{1,0:T(8,128)(2,1)} %bitcast.6, bf16[512,2304]{1,0:T(8,128)(2,1)} %bitcast.7), custom_call_target="tpu_custom_call" | custom-call | flops 40000000000 | bytes 20000000 | tf_op jit(solution)/shard_map/sublayer/pallas_call | solution.py:469
  187.1 3.2 %copy.8 = bf16[512,2304]{1,0:T(8,128)(2,1)} copy(bf16[512,2304]{1,0:T(8,128)(2,1)} %sublayer.1) | data formatting | bytes 4718592

commit v6 on v5

--- a/solution.py
+++ b/solution.py
@@ -397,34 +397,49 @@
     out_hop2_far()
     loads[4].wait()
 
-    def out_own(n, carry):
-        cols = rows(n, HD)
-        y32[:, cols] = jnp.dot(o_buf[z], wo_buf[0, :, cols], preferred_element_type=jnp.float32)
-        return carry
-
-    lax.fori_loop(0, d_model // HD, out_own, 0)
+    wide = 3 * HD
+
+    def out_add(o_ref, k, first):
+        def step(n, carry):
+            cols = rows(n, wide)
+            part = jnp.dot(o_ref[...], wo_buf[k, :, cols], preferred_element_type=jnp.float32)
+            y32[:, cols] = part if first else y32[:, cols] + part
+            return carry
+
+        lax.fori_loop(0, d_model // wide, step, 0)
+
+    out_add(o_buf.at[z], 0, True)
     out_hop3_far()
     out_wait(ONE, 1, 1)
     arrived(HOME + 1, o_recv.at[0])
-
-    def out_near(n, carry):
-        cols = rows(n, HD)
-        y32[:, cols] = y32[:, cols] + jnp.dot(o_recv[0], wo_buf[1, :, cols], preferred_element_type=jnp.float32)
+    out_add(o_recv.at[0], 1, False)
+    out_wait(TWO, 2, 2)
+
+    @pl.when(is_inner)
+    def _():
+        arrived(HOME + 3, o_recv.at[2])
+
+    @pl.when(is_edge)
+    def _():
+        arrived(HOME + 2, o_recv.at[1])
+
+    out_add(o_recv.at[1 + inner], 2 + inner, False)
+
+    @pl.when(is_inner)
+    def _():
+        arrived(HOME + 2, o_recv.at[1])
+
+    @pl.when(is_edge)
+    def _():
+        arrived(HOME + 3, o_recv.at[2])
+
+    def out_last(n, carry):
+        cols = rows(n, wide)
+        part = jnp.dot(o_recv[2 - inner], wo_buf[3 - inner, :, cols], preferred_element_type=jnp.float32)
+        y_ref[:, cols] = (y32[:, cols] + part).astype(jnp.bfloat16)
         return carry
 
-    lax.fori_loop(0, d_model // HD, out_near, 0)
-    out_wait(TWO, 2, 2)
-    for k in range(2, 4):
-        arrived(HOME + k, o_recv.at[k - 1])
-
-    def out_far(n, carry):
-        cols = rows(n, HD)
-        far = jnp.dot(o_recv[1], wo_buf[2, :, cols], preferred_element_type=jnp.float32)
-        far = far + jnp.dot(o_recv[2], wo_buf[3, :, cols], preferred_element_type=jnp.float32)
-        y_ref[:, cols] = (y32[:, cols] + far).astype(jnp.bfloat16)
-        return carry
-
-    lax.fori_loop(0, d_model // HD, out_far, 0)
+    lax.fori_loop(0, d_model // wide, out_last, 0)
 
     @pl.when(is_edge)
     def _():

time: 190 us -> 189 us (level)
  Pallas kernels: 184 us -> 182 us
where the time goes in v6:
time: 189 us
  Pallas kernels  182 us (96%)
  local copies, waits for them, and re-layouts  6.68 us (4%)
    pallas_call x1, Pallas kernels, local_attn(): pl.pallas_call(sublayer_kernel, out_shape=jax.ShapeDtypeStruct((HB, d_mod...  182 us
    unnamed x2, local copies, waits for them, and re-layouts  6.68 us

profile of v6, /device:TPU:26, one launch (start us, length us, event | category | flops | bytes accessed | tf_op | source)
XLA Modules:
  0.0 188.8 jit_solution(7999166365828980200)
XLA Ops:
  0.0 3.5 %copy.6 = bf16[288,8,2,256]{3,1,2,0:T(8,128)(2,1)} copy(bf16[288,8,2,256]{3,2,1,0:T(2,128)(2,1)} %bitcast.5) | data formatting | bytes 4718592
  3.5 182.1 %sublayer.1 = bf16[512,2304]{1,0:T(8,128)(2,1)} custom-call(bf16[512,2304]{1,0:T(8,128)(2,1)} %x_ref.1, bf16[2304,256]{1,0:T(8,128)(2,1)} %bitcast.8, bf16[2304,256]{1,0:T(8,128)(2,1)} %bitcast.9, bf16[2304,512]{1,0:T(8,128)(2,1)} %bitcast.6, bf16[512,2304]{1,0:T(8,128)(2,1)} %bitcast.7), custom_call_target="tpu_custom_call" | custom-call | flops 40000000000 | bytes 20000000 | tf_op jit(solution)/shard_map/sublayer/pallas_call | solution.py:484
  185.6 3.2 %copy.8 = bf16[512,2304]{1,0:T(8,128)(2,1)} copy(bf16[512,2304]{1,0:T(8,128)(2,1)} %sublayer.1) | data formatting | bytes 4718592
